TPU v7x, 256 devices: a whole 4x4x8 slice. The times are simulated.
256 devices in a mesh: datb: 8 (over z), model: 4 (over y), data: 8 (over x, core).
Axes of the slice: x: 4, y: 4, z: 8, core: 2. Of those that a mesh axis runs over, the one named last changes fastest.
Arguments:
- tokens: bfloat16 [16384, 2048], P(('datb', 'data', 'model'))
- w_gate: bfloat16 [2048, 16384], P(('datb', 'data'), 'model')
- w_up: bfloat16 [2048, 16384], P(('datb', 'data'), 'model')
- w_down: bfloat16 [16384, 2048], P('model', ('datb', 'data'))
- grad_out: bfloat16 [16384, 2048], P(('datb', 'data', 'model'))
Outputs:
- output 1: bfloat16 [16384, 2048], P(('datb', 'data', 'model'))
- output 2: bfloat16 [16384, 2048], P(('datb', 'data', 'model'))
- output 3: float32 [2048, 16384], P(('datb', 'data'), 'model')
- output 4: float32 [2048, 16384], P(('datb', 'data'), 'model')
- output 5: float32 [16384, 2048], P('model', ('datb', 'data'))
All inputs are finite; a program needn't handle non-finite values.
Results may differ from a plain program's by a relative error of at most 0.02.
Values are sent between devices in bfloat16 or wider.
A program may use at most 768 MiB of HBM per device.

v0:
```python
import jax
import jax.numpy as jnp
from jax import lax
from jax.sharding import PartitionSpec as P

ROW_SPEC = P(("datb", "data", "model"), None)
GATE_SPEC = P(("datb", "data"), "model")
DOWN_SPEC = P("model", ("datb", "data"))


def solution(mesh):
    datb_size = mesh.shape["datb"]
    data_size = mesh.shape["data"]
    model_size = mesh.shape["model"]

    def local_step(tok_loc, wg_loc, wu_loc, wd_loc, grad_loc):
        rows_dev, d_model = tok_loc.shape
        d_part = wg_loc.shape[0]
        shard_rows = rows_dev * model_size

        def to_rows(part_out):
            per_model = lax.psum_scatter(part_out.reshape(data_size, model_size, rows_dev, datb_size, d_part), "model", scatter_dimension=1)
            moved_rows = lax.all_to_all(per_model[:, :, :, None, :], "data", 0, 3, tiled=True)
            return moved_rows.reshape(rows_dev, d_model)

        gate_w = lax.all_gather(wg_loc, "datb", axis=0)
        up_w = lax.all_gather(wu_loc, "datb", axis=0)
        down_w = lax.all_gather(wd_loc, "datb", axis=1)

        tok_full = lax.all_gather(tok_loc, "model", axis=0, tiled=True)
        tok_split = lax.all_to_all(tok_full.reshape(shard_rows, datb_size, data_size, d_part), "data", 2, 2, tiled=True)
        gate_part = jnp.einsum("tbae,bef->taf", tok_split, gate_w, preferred_element_type=jnp.float32).astype(jnp.bfloat16)
        up_part = jnp.einsum("tbae,bef->taf", tok_split, up_w, preferred_element_type=jnp.float32).astype(jnp.bfloat16)
        gate_pre = lax.psum_scatter(gate_part, "data", scatter_dimension=1).astype(jnp.float32)
        up_pre = lax.psum_scatter(up_part, "data", scatter_dimension=1).astype(jnp.float32)
        gate_sig = jax.nn.sigmoid(gate_pre)
        silu_gate = gate_pre * gate_sig
        hidden = (silu_gate * up_pre).astype(jnp.bfloat16)
        hid_all = lax.all_gather(hidden, "data", axis=0)
        down_part = jnp.einsum("atf,fbe->atbe", hid_all, down_w, preferred_element_type=jnp.float32).astype(jnp.bfloat16)
        out = (tok_loc.astype(jnp.float32) + to_rows(down_part).astype(jnp.float32)).astype(jnp.bfloat16)

        grad_full = lax.all_gather(grad_loc, "model", axis=0, tiled=True)
        grad_split = lax.all_to_all(grad_full.reshape(shard_rows, datb_size, data_size, d_part), "data", 2, 2, tiled=True)
        grad_hid_part = jnp.einsum("tbae,fbe->taf", grad_split, down_w, preferred_element_type=jnp.float32).astype(jnp.bfloat16)
        grad_hidden = lax.psum_scatter(grad_hid_part, "data", scatter_dimension=1).astype(jnp.float32)
        grad_gate_pre = (grad_hidden * up_pre * gate_sig * (1.0 + gate_pre * (1.0 - gate_sig))).astype(jnp.bfloat16)
        grad_up_pre = (grad_hidden * silu_gate).astype(jnp.bfloat16)
        dgate_all = lax.all_gather(grad_gate_pre, "data", axis=0)
        dup_all = lax.all_gather(grad_up_pre, "data", axis=0)
        back_part = (jnp.einsum("atf,bef->atbe", dgate_all, gate_w, preferred_element_type=jnp.float32) + jnp.einsum("atf,bef->atbe", dup_all, up_w, preferred_element_type=jnp.float32)).astype(jnp.bfloat16)
        grad_in = (grad_loc.astype(jnp.float32) + to_rows(back_part).astype(jnp.float32)).astype(jnp.bfloat16)

        grad_down = lax.psum_scatter(jnp.einsum("atf,tbae->fbe", hid_all, grad_split, preferred_element_type=jnp.float32), "datb", scatter_dimension=1)
        grad_gate = lax.psum_scatter(jnp.einsum("tbae,atf->bef", tok_split, dgate_all, preferred_element_type=jnp.float32), "datb", scatter_dimension=0)
        grad_up = lax.psum_scatter(jnp.einsum("tbae,atf->bef", tok_split, dup_all, preferred_element_type=jnp.float32), "datb", scatter_dimension=0)
        return out, grad_in, grad_gate, grad_up, grad_down

    return jax.shard_map(local_step, mesh=mesh, in_specs=(ROW_SPEC, GATE_SPEC, GATE_SPEC, DOWN_SPEC, ROW_SPEC), out_specs=(ROW_SPEC, ROW_SPEC, GATE_SPEC, GATE_SPEC, DOWN_SPEC), check_vma=False)
```

profile of v0, /device:TPU:1, one launch (start us, length us, event | category | flops | bytes accessed | tf_op | source)
XLA Modules:
  0.0 1046.9 jit_solution(6417016050342745073)
XLA Ops:
  10.0 27.9 %all-gather.12.cloned.1.call-done = bf16[256,2048]{1,0:T(8,128)(2,1)} async-done(((bf16[64,2048]{1,0:T(8,128)(2,1)}), bf16[256,2048]{1,0:T(8,128)(2,1)}) %all-gather.12.cloned.1.call-update) | async-done | bytes 1048592 | tf_op jit(solution)/shard_map/all_gather | solution.py:30
  48.2 14.1 %all-to-all-done = bf16[256,8,8,32]{0,3,1,2:T(8,128)(2,1)S(1)} async-done(((bf16[256,8,8,32]{0,3,1,2:T(8,128)(2,1)}), bf16[256,8,8,32]{0,3,1,2:T(8,128)(2,1)S(1)}, u32[]{:S(2)}, u32[]{:S(2)}) %all-to-all-start) | async-done | bytes 1048608 | tf_op jit(solution)/shard_map/all_to_all | solution.py:31
  62.3 16.4 %all-gather.24.cloned.1.call-done = bf16[256,4096]{1,0:T(8,128)(2,1)} async-done(((bf16[32,4096]{1,0:T(8,128)(2,1)}), bf16[256,4096]{1,0:T(8,128)(2,1)}) %all-gather.24.cloned.1.call-update) | async-done | bytes 2097168 | tf_op jit(solution)/shard_map/all_gather | solution.py:27
  78.8 9.7 bitcast_convert_fusion.1
  88.6 31.2 %all-gather.22.cloned.1.call-done = bf16[256,4096]{1,0:T(8,128)(2,1)} async-done(((bf16[32,4096]{1,0:T(8,128)(2,1)}), bf16[256,4096]{1,0:T(8,128)(2,1)}) %all-gather.22.cloned.1.call-update) | async-done | bytes 2097168 | tf_op jit(solution)/shard_map/all_gather | solution.py:26
  119.8 9.7 bitcast_convert_fusion.2
  129.6 18.9 %all-gather.16.cloned.1.call-done = bf16[256,2048]{1,0:T(8,128)(2,1)} async-done(((bf16[64,2048]{1,0:T(8,128)(2,1)}), bf16[256,2048]{1,0:T(8,128)(2,1)}) %all-gather.16.cloned.1.call-update) | async-done | bytes 1048592 | tf_op jit(solution)/shard_map/all_gather | solution.py:43
  150.0 21.9 %all_to_all.28 = bf16[256,8,8,32]{0,3,1,2:T(8,128)(2,1)S(1)} all-to-all(bf16[256,8,8,32]{0,3,1,2:T(8,128)(2,1)S(1)} %copy.37), channel_id=1, replica_groups=mesh['datb'=8,'model'=4,'data'=8] {'data'}, dimensions={2} | all-to-all | bytes 2097152 | tf_op jit(solution)/shard_map/all_to_all | solution.py:44
  171.9 17.3 %all-gather.26.cloned.1.call-done = bf16[4096,256]{0,1:T(8,128)(2,1)} async-done(((bf16[4096,32]{0,1:T(8,128)(2,1)}), bf16[4096,256]{0,1:T(8,128)(2,1)}) %all-gather.26.cloned.1.call-update) | async-done | bytes 2097168 | tf_op jit(solution)/shard_map/all_gather | solution.py:28
  199.0 89.4 %reduce-scatter.11.cloned.1.call-done = bf16[256,1,4096]{2,0,1:T(8,128)(2,1)} async-done(((bf16[256,8,4096]{2,0,1:T(8,128)(2,1)}), bf16[256,1,4096]{2,0,1:T(8,128)(2,1)}) %reduce-scatter.11.cloned.1.call-update) | async-done | bytes 2097168 | tf_op jit(solution)/shard_map/reduce_scatter | solution.py:35
  288.4 96.7 %reduce-scatter.9.cloned.1.call-done = bf16[256,1,4096]{2,0,1:T(8,128)(2,1)} async-done(((bf16[256,8,4096]{2,0,1:T(8,128)(2,1)}), bf16[256,1,4096]{2,0,1:T(8,128)(2,1)}) %reduce-scatter.9.cloned.1.call-update) | async-done | bytes 2097168 | tf_op jit(solution)/shard_map/reduce_scatter | solution.py:34
  385.1 96.7 %reduce-scatter.13.cloned.1.call-done = bf16[256,1,4096]{2,0,1:T(8,128)(2,1)} async-done(((bf16[256,8,4096]{2,0,1:T(8,128)(2,1)}), bf16[256,1,4096]{2,0,1:T(8,128)(2,1)}) %reduce-scatter.13.cloned.1.call-update) | async-done | bytes 2097168 | tf_op jit(solution)/shard_map/reduce_scatter | solution.py:46
  489.5 86.9 %all-gather.20.cloned.1.call-done = bf16[8,256,4096]{2,1,0:T(8,128)(2,1)} async-done(((bf16[1,256,4096]{2,1,0:T(8,128)(2,1)}), bf16[8,256,4096]{2,1,0:T(8,128)(2,1)}) %all-gather.20.cloned.1.call-update) | async-done | bytes 16777232 | tf_op jit(solution)/shard_map/all_gather | solution.py:50
  585.8 80.6 %all-gather.18.cloned.1.call-done = bf16[8,256,4096]{2,1,0:T(8,128)(2,1)} async-done(((bf16[1,256,4096]{2,1,0:T(8,128)(2,1)}), bf16[8,256,4096]{2,1,0:T(8,128)(2,1)}) %all-gather.18.cloned.1.call-update) | async-done | bytes 16777232 | tf_op jit(solution)/shard_map/all_gather | solution.py:49
  666.4 11.5 %add_convert_fusion = bf16[8,256,8,32]{1,3,2,0:T(8,128)(2,1)S(1)} fusion(f32[8,256,8,32]{1,3,2,0:T(8,128)} %fusion.2, bf16[8,32,4096,1]{2,1,0,3:T(8,128)(2,1)} %bitcast.163, bf16[8,256,4096]{2,1,0:T(8,128)(2,1)} %all-gather.18.cloned.1.call-done), kind=kOutput, calls=%fused_computation.33 | convolution fusion | flops 4296015872 | bytes 22020096 | tf_op jit(solution)/shard_map/atf,bef->atbe/dot_general | solution.py:51
  680.6 76.0 %all-gather.14.cloned.1.call-done = bf16[8,256,4096]{2,1,0:T(8,128)(2,1)} async-done(((bf16[1,256,4096]{2,1,0:T(8,128)(2,1)}), bf16[8,256,4096]{2,1,0:T(8,128)(2,1)}) %all-gather.14.cloned.1.call-update) | async-done | bytes 16777232 | tf_op jit(solution)/shard_map/all_gather | solution.py:39
  756.5 10.9 %fusion.30 = bf16[8,256,8,32]{1,3,2,0:T(8,128)(2,1)S(1)} fusion(bf16[4096,8,32,1]{0,2,1,3:T(8,128)(2,1)} %bitcast.165, bf16[8,256,4096]{2,1,0:T(8,128)(2,1)} %all-gather.14.cloned.1.call-done), kind=kOutput, calls=%fused_computation.34 | convolution fusion | flops 4295491584 | bytes 19922944 | tf_op jit(solution)/shard_map/atf,fbe->atbe/dot_general | solution.py:40
  770.5 10.2 fusion.12
  781.9 10.2 fusion.15
  792.2 10.2 fusion.18
  803.7 64.4 %all-reduce.5.cloned.1.call-done = (bf16[8,4,64,8,32]{2,4,3,1,0:T(8,128)(2,1)}, bf16[8,4,64,8,32]{2,4,3,1,0:T(8,128)(2,1)}) async-done(((bf16[8,4,64,8,32]{2,4,3,1,0:T(8,128)(2,1)}, bf16[8,4,64,8,32]{2,4,3,1,0:T(8,128)(2,1)}), (bf16[8,4,64,8,32]{2,4,3,1,0:T(8,128)(2,1)}, bf16[8,4,64,8,32]{2,4,3,1,0:T(8,128)(2,1)})) %all-reduce.5.cloned.1.call-update) | async-done | bytes 2097168
  895.0 31.5 %reduce-scatter.19.cloned.1.call-done = f32[4096,1,32]{0,2,1:T(8,128)} async-done(((f32[4096,8,32]{0,2,1:T(8,128)}), f32[4096,1,32]{0,2,1:T(8,128)}) %reduce-scatter.19.cloned.1.call-update) | async-done | bytes 524304 | tf_op jit(solution)/shard_map/reduce_scatter | solution.py:54
  926.4 57.0 %reduce-scatter.15.cloned.1.call-done = f32[1,32,4096]{2,1,0:T(8,128)} async-done(((f32[8,32,4096]{2,1,0:T(8,128)}), f32[1,32,4096]{2,1,0:T(8,128)}) %reduce-scatter.15.cloned.1.call-update) | async-done | bytes 524304 | tf_op jit(solution)/shard_map/reduce_scatter | solution.py:55
  983.4 57.0 %reduce-scatter.17.cloned.1.call-done = f32[1,32,4096]{2,1,0:T(8,128)} async-done(((f32[8,32,4096]{2,1,0:T(8,128)}), f32[1,32,4096]{2,1,0:T(8,128)}) %reduce-scatter.17.cloned.1.call-update) | async-done | bytes 524304 | tf_op jit(solution)/shard_map/reduce_scatter | solution.py:56
  (78 shorter events, 76.6 us)
Async XLA Ops:
  7.2 30.7 %all-gather.12.cloned.1.call-start = ((), (), s32[]{:S(2)}) async-start(), calls=%async_computation.10 | async-start | bytes 1310720 | tf_op jit(solution)/shard_map/all_gather | solution.py:30
  7.9 70.9 %all-gather.24.cloned.1.call-start = ((), (), s32[]{:S(2)}) async-start(), calls=%async_computation.22 | async-start | bytes 2359296 | tf_op jit(solution)/shard_map/all_gather | solution.py:27
  8.6 111.2 %all-gather.22.cloned.1.call-start = ((), (), s32[]{:S(2)}) async-start(), calls=%async_computation.21 | async-start | bytes 2359296 | tf_op jit(solution)/shard_map/all_gather | solution.py:26
  9.4 139.1 %all-gather.16.cloned.1.call-start = ((), (), s32[]{:S(2)}) async-start(), calls=%async_computation.14 | async-start | bytes 1310720 | tf_op jit(solution)/shard_map/all_gather | solution.py:43
  40.4 21.9 %all-to-all-start = ((bf16[256,8,8,32]{0,3,1,2:T(8,128)(2,1)}), bf16[256,8,8,32]{0,3,1,2:T(8,128)(2,1)S(1)}, u32[]{:S(2)}, u32[]{:S(2)}) async-start(bf16[256,8,8,32]{0,3,1,2:T(8,128)(2,1)} %copy.32), calls=%async_computation | async-start | bytes 2097152 | tf_op jit(solution)/shard_map/all_to_all | solution.py:31
  47.6 141.7 %all-gather.26.cloned.1.call-start = ((), (), s32[]{:S(2)}) async-start(), calls=%async_computation.23 | async-start | bytes 2359296 | tf_op jit(solution)/shard_map/all_gather | solution.py:28
  48.2 240.2 %reduce-scatter.11.cloned.1.call-start = ((), (), s32[]{:S(2)}) async-start(), calls=%async_computation.12 | async-start | bytes 18874368 | tf_op jit(solution)/shard_map/reduce_scatter | solution.py:35
  62.3 57.5 %copy-start.2 = (bf16[256,8,8,32]{0,3,1,2:T(8,128)(2,1)}, bf16[256,8,8,32]{0,3,1,2:T(8,128)(2,1)S(1)}, u32[]{:S(2)}) copy-start(bf16[256,8,8,32]{0,3,1,2:T(8,128)(2,1)S(1)} %all-to-all-done) | copy-start | bytes 3145732
  88.5 296.5 %reduce-scatter.9.cloned.1.call-start = ((), (), s32[]{:S(2)}) async-start(), calls=%async_computation.11 | async-start | bytes 18874368 | tf_op jit(solution)/shard_map/reduce_scatter | solution.py:34
  129.5 352.3 %reduce-scatter.13.cloned.1.call-start = ((), (), s32[]{:S(2)}) async-start(), calls=%async_computation.15 | async-start | bytes 18874368 | tf_op jit(solution)/shard_map/reduce_scatter | solution.py:46
  171.9 27.0 %copy-start.4 = (bf16[256,8,8,32]{0,3,1,2:T(8,128)(2,1)}, bf16[256,8,8,32]{0,3,1,2:T(8,128)(2,1)S(1)}, u32[]{:S(2)}) copy-start(bf16[256,8,8,32]{0,3,1,2:T(8,128)(2,1)S(1)} %all_to_all.28) | copy-start | bytes 3145732
  199.0 377.4 %all-gather.20.cloned.1.call-start = ((), (), s32[]{:S(2)}) async-start(), calls=%async_computation.17 | async-start | bytes 18874368 | tf_op jit(solution)/shard_map/all_gather | solution.py:50
  487.9 88.4 %copy-start.6 = (bf16[256,4096]{1,0:T(8,128)(2,1)S(1)}, bf16[256,4096]{1,0:T(8,128)(2,1)}, u32[]{:S(2)}) copy-start(bf16[256,4096]{1,0:T(8,128)(2,1)} %all-gather.24.cloned.1.call-done) | copy-start | bytes 6291460
  487.9 178.4 %all-gather.18.cloned.1.call-start = ((), (), s32[]{:S(2)}) async-start(), calls=%async_computation.16 | async-start | bytes 18874368 | tf_op jit(solution)/shard_map/all_gather | solution.py:49
  488.5 268.0 %all-gather.14.cloned.1.call-start = ((), (), s32[]{:S(2)}) async-start(), calls=%async_computation.13 | async-start | bytes 18874368 | tf_op jit(solution)/shard_map/all_gather | solution.py:39
  489.2 378.8 %all-reduce.5.cloned.1.call-start = ((), (), s32[]{:S(2)}) async-start(), calls=%async_computation.24 | async-start | bytes 8388608
  768.3 2.2 copy-start.5
  770.2 156.2 %reduce-scatter.19.cloned.1.call-start = ((), (), s32[]{:S(2)}) async-start(), calls=%async_computation.20 | async-start | bytes 4718592 | tf_op jit(solution)/shard_map/reduce_scatter | solution.py:54
  780.7 202.7 %reduce-scatter.15.cloned.1.call-start = ((), (), s32[]{:S(2)}) async-start(), calls=%async_computation.18 | async-start | bytes 4718592 | tf_op jit(solution)/shard_map/reduce_scatter | solution.py:55
  792.1 248.2 %reduce-scatter.17.cloned.1.call-start = ((), (), s32[]{:S(2)}) async-start(), calls=%async_computation.19 | async-start | bytes 4718592 | tf_op jit(solution)/shard_map/reduce_scatter | solution.py:56
  802.4 73.9 %copy-start = (bf16[64,2048]{1,0:T(8,128)(2,1)S(1)}, bf16[64,2048]{1,0:T(8,128)(2,1)}, u32[]{:S(2)}) copy-start(bf16[64,2048]{1,0:T(8,128)(2,1)} %param.5) | copy-start | bytes 786436
  802.4 74.2 %copy-start.1 = (bf16[64,2048]{1,0:T(8,128)(2,1)S(1)}, bf16[64,2048]{1,0:T(8,128)(2,1)}, u32[]{:S(2)}) copy-start(bf16[64,2048]{1,0:T(8,128)(2,1)} %param.9) | copy-start | bytes 786436
  871.1 11.5 %all-to-all-start.1 = ((bf16[8,2,8192]{2,1,0:T(2,128)(2,1)}), bf16[8,2,8192]{2,1,0:T(2,128)(2,1)S(1)}, u32[]{:S(2)}, u32[]{:S(2)}) async-start(bf16[8,2,8192]{2,1,0:T(2,128)(2,1)} %reshape.166), calls=%async_computation.3 | async-start | bytes 524288 | tf_op jit(solution)/shard_map/all_to_all | solution.py:23
  882.6 10.8 %all-to-all-start.3 = ((bf16[8,2,8192]{2,1,0:T(2,128)(2,1)}), bf16[8,2,8192]{2,1,0:T(2,128)(2,1)S(1)}, u32[]{:S(2)}, u32[]{:S(2)}) async-start(bf16[8,2,8192]{2,1,0:T(2,128)(2,1)} %reshape.168), calls=%async_computation.6 | async-start | bytes 524288 | tf_op jit(solution)/shard_map/all_to_all | solution.py:23
  (2 other events, 1.9 us)
Sparse Core Ops, SparseCore 0:
  9.8 28.0 all-gather.11
  39.6 39.1 all-gather.23
  80.6 39.1 all-gather.21
  121.5 26.9 all-gather.15
  150.1 39.0 all-gather.25
  191.7 96.6 reduce-scatter.10
  291.0 94.0 reduce-scatter.8
  387.7 94.0 reduce-scatter.12
  488.0 88.2 all-gather.19
  578.0 88.2 all-gather.17
  668.2 88.2 all-gather.13
  770.3 97.6 all-reduce.4
  871.2 55.1 reduce-scatter.18
  929.4 53.9 reduce-scatter.14
  986.4 53.9 reduce-scatter.16
where the time goes:
time: 1050 us
  waiting for transfers between devices  876 us (83%)
  matrix products  91.6 us (9%)
  blocking collectives  21.9 us (2%)
  local copies, waits for them, and re-layouts  19.3 us (2%)
  starting transfers between devices  17.7 us (2%)
  between operations  14.1 us (1%)
    reduce_scatter x1, waiting for transfers between devices, local_step(): lax.psum_scatter(gate_part, 'data', scatter_dimension=1).astype(jnp.float32)  96.7 us
    reduce_scatter x1, waiting for transfers between devices, local_step(): lax.psum_scatter(grad_hid_part, 'data', scatter_dimension=1)  96.7 us
    reduce_scatter x1, waiting for transfers between devices, local_step(): lax.psum_scatter(up_part, 'data', scatter_dimension=1).astype(jnp.float32)  89.4 us
    all_gather x1, waiting for transfers between devices, local_step(): dup_all = lax.all_gather(grad_up_pre, 'data', axis=0)  86.9 us
    all_gather x1, waiting for transfers between devices, local_step(): dgate_all = lax.all_gather(grad_gate_pre, 'data', axis=0)  80.6 us
    all_gather x1, waiting for transfers between devices, local_step(): hid_all = lax.all_gather(hidden, 'data', axis=0)  76 us
    unnamed x16, waiting for transfers between devices  68.9 us
    reduce_scatter x1, waiting for transfers between devices, local_step(): lax.psum_scatter(jnp.einsum('tbae,atf->bef', tok_split, dgate_all, prefer...  57 us
  transfers between devices with their start and end apart: 18, of which 18 were waited for; matrix products, arithmetic and copies ran while one was open for 9% of the time, Pallas kernels for 0%

commit v1 on v0

v1 whole, which is shorter than its diff:
```python
import jax
import jax.numpy as jnp
from jax import lax
from jax.sharding import PartitionSpec as P

ROW_SPEC = P(("datb", "data", "model"), None)
GATE_SPEC = P(("datb", "data"), "model")
DOWN_SPEC = P("model", ("datb", "data"))


def dot(lhs, rhs, ldim, rdim):
    return lax.dot_general(lhs, rhs, (((ldim,), (rdim,)), ((), ())), preferred_element_type=jnp.float32)


def solution(mesh):
    data_size = mesh.shape["data"]

    def local_step(tok_loc, wg_loc, wu_loc, wd_loc, grad_loc):
        d_part, f_part = wg_loc.shape
        f_own = f_part // data_size

        mine = jnp.stack([wg_loc, wu_loc, wd_loc.T]).reshape(3, d_part, data_size, f_own)
        mine = lax.all_to_all(mine, "data", 2, 1, tiled=False)
        mine = mine.reshape(3, d_part * data_size, f_own)

        tok = lax.all_gather(tok_loc, ("data", "model"), axis=0, tiled=True)
        gate_w = lax.all_gather(mine[0], "datb", axis=0, tiled=True)
        up_w = lax.all_gather(mine[1], "datb", axis=0, tiled=True)
        grad = lax.all_gather(grad_loc, ("data", "model"), axis=0, tiled=True)
        down_w = lax.all_gather(mine[2], "datb", axis=0, tiled=True)

        gate_pre = dot(tok, gate_w, 1, 0).astype(jnp.bfloat16).astype(jnp.float32)
        up_pre = dot(tok, up_w, 1, 0).astype(jnp.bfloat16).astype(jnp.float32)
        gate_sig = jax.nn.sigmoid(gate_pre)
        silu_gate = gate_pre * gate_sig
        hidden = (silu_gate * up_pre).astype(jnp.bfloat16)

        def home(part):
            moved = lax.psum_scatter(part, "datb", scatter_dimension=0, tiled=True)
            moved = moved.reshape(data_size, d_part, f_own)
            return lax.all_to_all(moved, "data", 0, 1, tiled=False).reshape(d_part, f_part)

        grad_down = home(dot(grad, hidden, 0, 0)).T
        grad_hidden = dot(grad, down_w, 1, 0).astype(jnp.bfloat16).astype(jnp.float32)
        grad_gate_pre = (grad_hidden * up_pre * gate_sig * (1.0 + gate_pre * (1.0 - gate_sig))).astype(jnp.bfloat16)
        grad_up_pre = (grad_hidden * silu_gate).astype(jnp.bfloat16)
        grad_gate = home(dot(tok, grad_gate_pre, 0, 0))
        grad_up = home(dot(tok, grad_up_pre, 0, 0))

        down_part = dot(hidden, down_w, 1, 1).astype(jnp.bfloat16)
        back_part = (dot(grad_gate_pre, gate_w, 1, 1) + dot(grad_up_pre, up_w, 1, 1)).astype(jnp.bfloat16)
        down_sum = lax.psum_scatter(down_part, ("data", "model"), scatter_dimension=0, tiled=True)
        back_sum = lax.psum_scatter(back_part, ("data", "model"), scatter_dimension=0, tiled=True)
        out = (tok_loc.astype(jnp.float32) + down_sum.astype(jnp.float32)).astype(jnp.bfloat16)
        grad_in = (grad_loc.astype(jnp.float32) + back_sum.astype(jnp.float32)).astype(jnp.bfloat16)
        return out, grad_in, grad_gate, grad_up, grad_down

    return jax.shard_map(local_step, mesh=mesh, in_specs=(ROW_SPEC, GATE_SPEC, GATE_SPEC, DOWN_SPEC, ROW_SPEC), out_specs=(ROW_SPEC, ROW_SPEC, GATE_SPEC, GATE_SPEC, DOWN_SPEC), check_vma=False)
```

time: 1050 us -> 668 us (0.64)
  waiting for transfers between devices: 876 us -> 483 us
    reduce_scatter x6 -> x5, waiting for transfers between devices: 428 us -> 266 us  [the longest x1 102 us: local_step(): lax.psum_scatter(back_part, ('data', 'model'), scatter_dimension=0, tiled...]
    all_gather x8 -> x5, waiting for transfers between devices: 355 us -> 208 us  [the longest x1 63.2 us: local_step(): tok = lax.all_gather(tok_loc, ('data', 'model'), axis=0, tiled=True)]
    unnamed x16 -> x10, waiting for transfers between devices: 68.9 us -> 2.53 us
    all_to_all x3, waiting for transfers between devices: 23.5 us -> 7.48 us  [home(): lax.all_to_all(moved, 'data', 0, 1, tiled=False).reshape(d_part, f_part)]
  transfers between devices with their start and end apart: 18 -> 13, of which waited for: 18 -> 10; matrix products, arithmetic and copies ran while one was open for 9% -> 17% of each run, Pallas kernels for 0% -> 0%
where the time goes in v1:
time: 668 us; the launch traced here: 657 us
  waiting for transfers between devices  483 us (72%)
  matrix products  100 us (15%)
  starting transfers between devices  20.4 us (3%)
  blocking collectives  17.7 us (3%)
  local copies, waits for them, and re-layouts  17.1 us (3%)
  between operations  14.5 us (2%)
    reduce_scatter x1, waiting for transfers between devices, local_step(): lax.psum_scatter(back_part, ('data', 'model'), scatter_dimension=0, tiled...  102 us
    dot_general x9, matrix products, dot(): lax.dot_general(lhs, rhs, (((ldim,), (rdim,)), ((), ())), preferred_eleme...  100 us
    reduce_scatter x1, waiting for transfers between devices, local_step(): lax.psum_scatter(down_part, ('data', 'model'), scatter_dimension=0, tiled...  84.2 us
    reduce_scatter x3, waiting for transfers between devices, home(): moved = lax.psum_scatter(part, 'datb', scatter_dimension=0, tiled=True)  79.4 us
    all_gather x1, waiting for transfers between devices, local_step(): tok = lax.all_gather(tok_loc, ('data', 'model'), axis=0, tiled=True)  63.2 us
    all_gather x1, waiting for transfers between devices, local_step(): grad = lax.all_gather(grad_loc, ('data', 'model'), axis=0, tiled=True)  53.1 us
    all_gather x1, waiting for transfers between devices, local_step(): gate_w = lax.all_gather(mine[0], 'datb', axis=0, tiled=True)  35.4 us
    all_gather x1, waiting for transfers between devices, local_step(): up_w = lax.all_gather(mine[1], 'datb', axis=0, tiled=True)  29.5 us
  transfers between devices with their start and end apart: 13, of which 10 were waited for; matrix products, arithmetic and copies ran while one was open for 17% of the time, Pallas kernels for 0%

profile of v1, /device:TPU:1, one launch (start us, length us, event | category | flops | bytes accessed | tf_op | source)
XLA Modules:
  0.0 656.7 jit_solution(10867494502883287182)
XLA Ops:
  10.7 17.7 %all_to_all.60 = bf16[3,1,32,8,512]{4,2,1,0,3:T(8,128)(2,1)S(1)} all-to-all(bf16[3,1,32,8,512]{4,2,1,0,3:T(8,128)(2,1)S(1)} %copy.25), channel_id=1, replica_groups=mesh['datb'=8,'model'=4,'data'=8] {'data'}, dimensions={3} | all-to-all | bytes 1572864 | tf_op jit(solution)/shard_map/all_to_all | solution.py:23
  32.1 35.4 %all-gather.6.cloned.1.call-done = bf16[2048,512]{1,0:T(8,128)(2,1)} async-done(((bf16[256,512]{1,0:T(8,128)(2,1)}), bf16[2048,512]{1,0:T(8,128)(2,1)}) %all-gather.6.cloned.1.call-update) | async-done | bytes 2097168 | tf_op jit(solution)/shard_map/all_gather | solution.py:27
  67.5 63.2 %all-gather.8.cloned.1.call-done = bf16[2048,2048]{1,0:T(8,128)(2,1)} async-done(((bf16[64,2048]{1,0:T(8,128)(2,1)}), bf16[2048,2048]{1,0:T(8,128)(2,1)}) %all-gather.8.cloned.1.call-update) | async-done | bytes 8388624 | tf_op jit(solution)/shard_map/all_gather | solution.py:26
  130.7 8.6 %convolution_convert_fusion.3 = bf16[512,2048]{1,0:T(8,128)(2,1)S(1)} fusion(bf16[2048,512]{1,0:T(8,128)(2,1)} %all-gather.6.cloned.1.call-done, bf16[2048,2048]{1,0:T(8,128)(2,1)} %all-gather.8.cloned.1.call-done), kind=kOutput, calls=%fused_computation.22 | convolution fusion | flops 4296015872 | bytes 12582912 | tf_op jit(solution)/shard_map/dot_general | solution.py:12
  139.2 29.5 %all-gather.10.cloned.1.call-done = bf16[2048,512]{1,0:T(8,128)(2,1)} async-done(((bf16[256,512]{1,0:T(8,128)(2,1)}), bf16[2048,512]{1,0:T(8,128)(2,1)}) %all-gather.10.cloned.1.call-update) | async-done | bytes 2097168 | tf_op jit(solution)/shard_map/all_gather | solution.py:28
  168.7 9.9 %convolution_convert_fusion.2 = bf16[512,2048]{1,0:T(8,128)(2,1)} fusion(bf16[2048,512]{1,0:T(8,128)(2,1)} %all-gather.10.cloned.1.call-done, bf16[2048,2048]{1,0:T(8,128)(2,1)} %all-gather.8.cloned.1.call-done), kind=kOutput, calls=%fused_computation.21 | convolution fusion | flops 4296015872 | bytes 12582912 | tf_op jit(solution)/shard_map/dot_general | solution.py:12
  178.6 53.1 %all-gather.14.cloned.1.call-done = bf16[2048,2048]{1,0:T(8,128)(2,1)} async-done(((bf16[64,2048]{1,0:T(8,128)(2,1)}), bf16[2048,2048]{1,0:T(8,128)(2,1)}) %all-gather.14.cloned.1.call-update) | async-done | bytes 8388624 | tf_op jit(solution)/shard_map/all_gather | solution.py:29
  231.7 11.3 %convolution_bitcast_fusion = f32[2048,512]{0,1:T(8,128)} fusion(bf16[2048,2048]{1,0:T(8,128)(2,1)} %all-gather.14.cloned.1.call-done, bf16[512,2048]{1,0:T(8,128)(2,1)} %convolution_convert_fusion.2, bf16[512,2048]{1,0:T(8,128)(2,1)S(1)} %convolution_convert_fusion.3), kind=kOutput, calls=%fused_computation.17 | convolution fusion | flops 4303355904 | bytes 16777216 | tf_op jit(solution)/shard_map/dot_general | solution.py:12
  243.0 26.6 %all-gather.12.cloned.1.call-done = bf16[2048,512]{1,0:T(8,128)(2,1)} async-done(((bf16[256,512]{1,0:T(8,128)(2,1)}), bf16[2048,512]{1,0:T(8,128)(2,1)}) %all-gather.12.cloned.1.call-update) | async-done | bytes 2097168 | tf_op jit(solution)/shard_map/all_gather | solution.py:30
  269.6 8.7 %convolution_convert_fusion.1 = bf16[512,2048]{1,0:T(8,128)(2,1)S(1)} fusion(bf16[2048,512]{1,0:T(8,128)(2,1)} %all-gather.12.cloned.1.call-done, bf16[2048,2048]{1,0:T(8,128)(2,1)} %all-gather.14.cloned.1.call-done), kind=kOutput, calls=%fused_computation.20 | convolution fusion | flops 4296015872 | bytes 12582912 | tf_op jit(solution)/shard_map/dot_general | solution.py:12
  279.6 10.5 %convolution_bitcast_fusion.2 = f32[2048,512]{0,1:T(8,128)} fusion(bf16[2048,2048]{1,0:T(8,128)(2,1)} %all-gather.8.cloned.1.call-done, bf16[512,2048]{1,0:T(8,128)(2,1)S(1)} %convolution_convert_fusion.1, bf16[512,2048]{1,0:T(8,128)(2,1)S(1)} %copy-done.5, bf16[512,2048]{1,0:T(8,128)(2,1)S(1)} %convolution_convert_fusion.3), kind=kOutput, calls=%fused_computation.19 | convolution fusion | flops 4308598784 | bytes 18874368 | tf_op jit(solution)/shard_map/dot_general | solution.py:12
  290.2 10.8 %convolution_bitcast_fusion.1 = f32[2048,512]{0,1:T(8,128)} fusion(bf16[2048,2048]{1,0:T(8,128)(2,1)} %all-gather.8.cloned.1.call-done, bf16[512,2048]{1,0:T(8,128)(2,1)} %copy-done.6, bf16[512,2048]{1,0:T(8,128)(2,1)S(1)} %convolution_convert_fusion.3), kind=kOutput, calls=%fused_computation.18 | convolution fusion | flops 4303355904 | bytes 16777216 | tf_op jit(solution)/shard_map/dot_general | solution.py:12
  302.7 10.3 %convolution_convert_fusion = bf16[2048,2048]{1,0:T(8,128)(2,1)} fusion(bf16[2048,512]{1,0:T(8,128)(2,1)S(1)} %copy-done.3, bf16[512,2048]{1,0:T(8,128)(2,1)} %convolution_convert_fusion.2, bf16[512,2048]{1,0:T(8,128)(2,1)} %copy-done.4), kind=kOutput, calls=%fused_computation.1 | convolution fusion | flops 4307550208 | bytes 14680064 | tf_op jit(solution)/shard_map/dot_general | solution.py:12
  314.6 14.0 %fusion.14 = f32[2048,2048]{1,0:T(8,128)} fusion(bf16[2048,512]{1,0:T(8,128)(2,1)S(1)} %copy-done.2, bf16[512,2048]{1,0:T(8,128)(2,1)} %copy-done.6, bf16[512,2048]{1,0:T(8,128)(2,1)} %convolution_convert_fusion.2, bf16[512,2048]{1,0:T(8,128)(2,1)} %copy-done.4), kind=kOutput, calls=%fused_computation.27 | convolution fusion | flops 4308598784 | bytes 25165824 | tf_op jit(solution)/shard_map/dot_general | solution.py:12
  328.5 16.2 %add_convert_fusion = bf16[2048,2048]{1,0:T(8,128)(2,1)} fusion(f32[2048,2048]{1,0:T(8,128)} %fusion.14, bf16[2048,512]{1,0:T(8,128)(2,1)} %all-gather.10.cloned.1.call-done, bf16[512,2048]{1,0:T(8,128)(2,1)} %copy-done.6, bf16[512,2048]{1,0:T(8,128)(2,1)} %copy-done.4), kind=kOutput, calls=%fused_computation | convolution fusion | flops 4311744512 | bytes 31457280 | tf_op jit(solution)/shard_map/dot_general | solution.py:12
  344.8 2.0 copy.33
  346.9 9.4 %all-to-all-start.3 = ((f32[8,32,1,512]{3,1,2,0:T(8,128)}), f32[8,32,1,512]{3,1,2,0:T(8,128)S(1)}, u32[]{:S(2)}, u32[]{:S(2)}) async-start(f32[8,32,1,512]{3,1,2,0:T(8,128)} %bitcast.22), calls=%async_computation.8 | async-start | bytes 1048576 | tf_op jit(solution)/shard_map/all_to_all | solution.py:41
  356.3 30.0 %reduce-scatter.10.cloned.1.call-done = f32[256,512]{0,1:T(8,128)} async-done(((f32[2048,512]{0,1:T(8,128)}), f32[256,512]{0,1:T(8,128)}) %reduce-scatter.10.cloned.1.call-update) | async-done | bytes 524304 | tf_op jit(solution)/shard_map/reduce_scatter | solution.py:39
  388.4 5.2 all-to-all-start.1
  393.6 49.3 %reduce-scatter.12.cloned.1.call-done = f32[256,512]{0,1:T(8,128)} async-done(((f32[2048,512]{0,1:T(8,128)}), f32[256,512]{0,1:T(8,128)}) %reduce-scatter.12.cloned.1.call-update) | async-done | bytes 524304 | tf_op jit(solution)/shard_map/reduce_scatter | solution.py:39
  444.9 5.2 all-to-all-start.2
  451.8 7.5 %all-to-all-done.2 = f32[8,32,1,512]{3,1,2,0:T(8,128)S(1)} async-done(((f32[8,32,1,512]{3,1,2,0:T(8,128)}), f32[8,32,1,512]{3,1,2,0:T(8,128)S(1)}, u32[]{:S(2)}, u32[]{:S(2)}) %all-to-all-start.2) | async-done | bytes 524320 | tf_op jit(solution)/shard_map/all_to_all | solution.py:41
  460.1 84.2 %reduce-scatter.6.cloned.1.call-done = bf16[64,2048]{1,0:T(8,128)(2,1)} async-done(((bf16[2048,2048]{1,0:T(8,128)(2,1)}), bf16[64,2048]{1,0:T(8,128)(2,1)}) %reduce-scatter.6.cloned.1.call-update) | async-done | bytes 262160 | tf_op jit(solution)/shard_map/reduce_scatter | solution.py:52
  546.1 102.0 %reduce-scatter.8.cloned.1.call-done = bf16[64,2048]{1,0:T(8,128)(2,1)} async-done(((bf16[2048,2048]{1,0:T(8,128)(2,1)}), bf16[64,2048]{1,0:T(8,128)(2,1)}) %reduce-scatter.8.cloned.1.call-update) | async-done | bytes 262160 | tf_op jit(solution)/shard_map/reduce_scatter | solution.py:53
  (51 shorter events, 21.7 us)
Async XLA Ops:
  7.2 60.3 %all-gather.6.cloned.1.call-start = ((), (), s32[]{:S(2)}) async-start(), calls=%async_computation.9 | async-start | bytes 2359296 | tf_op jit(solution)/shard_map/all_gather | solution.py:27
  29.4 101.3 %all-gather.8.cloned.1.call-start = ((), (), s32[]{:S(2)}) async-start(), calls=%async_computation.10 | async-start | bytes 8650752 | tf_op jit(solution)/shard_map/all_gather | solution.py:26
  30.1 138.6 %all-gather.10.cloned.1.call-start = ((), (), s32[]{:S(2)}) async-start(), calls=%async_computation.11 | async-start | bytes 2359296 | tf_op jit(solution)/shard_map/all_gather | solution.py:28
  30.9 200.9 %all-gather.14.cloned.1.call-start = ((), (), s32[]{:S(2)}) async-start(), calls=%async_computation.14 | async-start | bytes 8650752 | tf_op jit(solution)/shard_map/all_gather | solution.py:29
  31.4 238.2 %all-gather.12.cloned.1.call-start = ((), (), s32[]{:S(2)}) async-start(), calls=%async_computation.12 | async-start | bytes 2359296 | tf_op jit(solution)/shard_map/all_gather | solution.py:30
  32.0 312.8 %reduce-scatter.14.cloned.1.call-start = ((), (), s32[]{:S(2)}) async-start(), calls=%async_computation.18 | async-start | bytes 4718592 | tf_op jit(solution)/shard_map/reduce_scatter | solution.py:39
  139.2 151.0 %copy-start.4 = (bf16[512,2048]{1,0:T(8,128)(2,1)}, bf16[512,2048]{1,0:T(8,128)(2,1)S(1)}, u32[]{:S(2)}) copy-start(bf16[512,2048]{1,0:T(8,128)(2,1)S(1)} %convolution_convert_fusion.3) | copy-start | bytes 6291460
  243.0 143.4 %reduce-scatter.10.cloned.1.call-start = ((), (), s32[]{:S(2)}) async-start(), calls=%async_computation.16 | async-start | bytes 4718592 | tf_op jit(solution)/shard_map/reduce_scatter | solution.py:39
  269.6 10.0 %copy-start.5 = (bf16[512,2048]{1,0:T(8,128)(2,1)S(1)}, bf16[512,2048]{1,0:T(8,128)(2,1)}, u32[]{:S(2)}) copy-start(bf16[512,2048]{1,0:T(8,128)(2,1)} %convolution_convert_fusion.2) | copy-start | bytes 6291460
  278.3 1.3 copy-start.6
  290.2 152.7 %reduce-scatter.12.cloned.1.call-start = ((), (), s32[]{:S(2)}) async-start(), calls=%async_computation.17 | async-start | bytes 4718592 | tf_op jit(solution)/shard_map/reduce_scatter | solution.py:39
  301.1 1.6 copy-start.3
  301.1 243.2 %reduce-scatter.6.cloned.1.call-start = ((), (), s32[]{:S(2)}) async-start(), calls=%async_computation.13 | async-start | bytes 8650752 | tf_op jit(solution)/shard_map/reduce_scatter | solution.py:52
  313.0 1.6 copy-start.2
  313.0 335.0 %reduce-scatter.8.cloned.1.call-start = ((), (), s32[]{:S(2)}) async-start(), calls=%async_computation.15 | async-start | bytes 8650752 | tf_op jit(solution)/shard_map/reduce_scatter | solution.py:53
  346.9 197.5 %copy-start = (bf16[64,2048]{1,0:T(8,128)(2,1)S(1)}, bf16[64,2048]{1,0:T(8,128)(2,1)}, u32[]{:S(2)}) copy-start(bf16[64,2048]{1,0:T(8,128)(2,1)} %param.5) | copy-start | bytes 786436
  346.9 41.5 %all-to-all-start.3 = ((f32[8,32,1,512]{3,1,2,0:T(8,128)}), f32[8,32,1,512]{3,1,2,0:T(8,128)S(1)}, u32[]{:S(2)}, u32[]{:S(2)}) async-start(f32[8,32,1,512]{3,1,2,0:T(8,128)} %bitcast.22), calls=%async_computation.8 | async-start | bytes 1048576 | tf_op jit(solution)/shard_map/all_to_all | solution.py:41
  356.3 291.7 %copy-start.1 = (bf16[64,2048]{1,0:T(8,128)(2,1)S(1)}, bf16[64,2048]{1,0:T(8,128)(2,1)}, u32[]{:S(2)}) copy-start(bf16[64,2048]{1,0:T(8,128)(2,1)} %param.9) | copy-start | bytes 786436
  388.4 56.5 %all-to-all-start.1 = ((f32[8,32,1,512]{3,1,2,0:T(8,128)}), f32[8,32,1,512]{3,1,2,0:T(8,128)S(1)}, u32[]{:S(2)}, u32[]{:S(2)}) async-start(f32[8,32,1,512]{3,1,2,0:T(8,128)} %bitcast.12), calls=%async_computation.4 | async-start | bytes 1048576 | tf_op jit(solution)/shard_map/all_to_all | solution.py:41
  444.9 14.3 %all-to-all-start.2 = ((f32[8,32,1,512]{3,1,2,0:T(8,128)}), f32[8,32,1,512]{3,1,2,0:T(8,128)S(1)}, u32[]{:S(2)}, u32[]{:S(2)}) async-start(f32[8,32,1,512]{3,1,2,0:T(8,128)} %bitcast.17), calls=%async_computation.6 | async-start | bytes 1048576 | tf_op jit(solution)/shard_map/all_to_all | solution.py:41
Sparse Core Ops, SparseCore 0:
  29.5 37.9 all-gather.5
  70.1 60.5 all-gather.7
  133.0 35.6 all-gather.9
  171.1 60.5 all-gather.13
  233.9 35.6 all-gather.11
  272.0 57.7 reduce-scatter.13
  332.4 53.9 reduce-scatter.9
  388.9 53.9 reduce-scatter.11
  446.9 97.3 reduce-scatter.5
  548.2 99.7 reduce-scatter.7

commit v2 on v1

v2 whole, which is shorter than its diff:
```python
import functools

import jax
import jax.numpy as jnp
from jax import lax
from jax.experimental import pallas as pl
from jax.experimental.pallas import tpu as pltpu
from jax.sharding import PartitionSpec as P

ROW_SPEC = P(("datb", "data", "model"), None)
GATE_SPEC = P(("datb", "data"), "model")
DOWN_SPEC = P("model", ("datb", "data"))
BF = jnp.bfloat16
F32 = jnp.float32
CORES = 2


def dot(lhs, rhs, ldim, rdim):
    return lax.dot_general(lhs, rhs, (((ldim,), (rdim,)), ((), ())), preferred_element_type=F32)


def sized(start, size):
    return pl.ds(pl.multiple_of(start, size), size)


def kernel(nz, ny, nx, tok_in, grad_in, wg_in, wu_in, wd_in, out_ref, gin_ref, dg_ref, du_ref, dd_ref,
           tok, grd, wgt, act, act_t, zrecv, zsend, ysum, stage, ya_recv, xa_recv, yb_recv, xb_recv,
           in_sem, a2a_s, a2a_r, ag_s, ag_r, p1_s, p1_r, p2_s, p2_r, pc_s, pc_r, rs_s, rs_r, credit,
           ex_s, ex_r, sa_s, sa_r, sb_s, sb_r, fa_s, fa_r):
    z, y, me = lax.axis_index("datb"), lax.axis_index("model"), lax.axis_index("data")
    x, c = me // CORES, lax.rem(me, CORES)
    nd = nx * CORES
    r, d_model = tok_in.shape
    dp, fp = wg_in.shape
    fo = fp // nd
    hf, zb, br = fo // 2, dp * nd, r * ny
    bh, rh = br // 2, r // 2

    z_to = ({"datb": lax.rem(z + 1, nz)}, {"datb": lax.rem(z + nz - 1, nz)})
    y_to = ({"model": lax.rem(y + 1, ny)}, {"model": lax.rem(y + ny - 1, ny)})
    x_to = ({"data": lax.rem(x + 1, nx) * CORES + c}, {"data": lax.rem(x + nx - 1, nx) * CORES + c})
    mate = {"data": x * CORES + 1 - c}

    def back(pos, n, d, s):
        return lax.rem(pos - s + 2 * n, n) if d == 0 else lax.rem(pos + s, n)

    def rcopy(src, dst, ss, rs, to):
        return pltpu.make_async_remote_copy(src_ref=src, dst_ref=dst, send_sem=ss, recv_sem=rs, device_id=to,
                                            device_id_type=pl.DeviceIdType.MESH)

    own = (tok.at[x, c, sized(y * r, r), :], grd.at[x, c, sized(y * r, r), :])
    w_in = (wg_in, wu_in, wd_in)
    moves = list(zip((tok_in, grad_in), own))
    moves += [(w_in[m].at[:, sized(me * fo, fo)], wgt.at[m, sized(z * zb + me * dp, dp), :]) for m in range(3)]
    loads = [pltpu.make_async_copy(src, dst, in_sem.at[i]) for i, (src, dst) in enumerate(moves)]
    for cp in loads:
        cp.start()
    barrier = pltpu.get_barrier_semaphore()
    peers = [{"data": lax.rem(me + k, nd)} for k in range(1, nd)]
    for to in peers + list(z_to) + list(y_to):
        pl.semaphore_signal(barrier, inc=1, device_id=to, device_id_type=pl.DeviceIdType.MESH)
    pl.semaphore_wait(barrier, nd - 1 + 4)

    def a2a(m, k):
        to = lax.rem(me + k, nd)
        return rcopy(w_in[m].at[:, sized(to * fo, fo)], wgt.at[m, sized(z * zb + me * dp, dp), :],
                     a2a_s.at[m, k - 1], a2a_r.at[m, k - 1], {"data": to})

    def a2a_wait(m, k):
        frm = lax.rem(me + nd - k, nd)
        dst = wgt.at[m, sized(z * zb + frm * dp, dp), :]
        rcopy(dst, dst, a2a_s.at[m, k - 1], a2a_r.at[m, k - 1], {"data": frm}).wait_recv()

    def ag_copy(m, d, s, pos):
        ref = wgt.at[m, sized(back(pos, nz, d, s) * zb, zb), pl.ds(d * hf, hf)]
        return rcopy(ref, ref, ag_s.at[m, d, s], ag_r.at[m, d, s], z_to[d])

    def ag_send(m, d, s):
        ag_copy(m, d, s, z).start()

    def ag_wait(m, d, s):
        ag_copy(m, d, s, z - 1 if d == 0 else z + 1).wait_recv()

    def p1_copy(arr, d, s, shift):
        if arr == 0:
            pos = y + shift
            ref = tok.at[x, c, sized(back(pos, ny, d, s) * r + d * rh, rh), :]
        else:
            pos = x + shift
            ref = grd.at[back(pos, nx, d, s), c, sized(y * r + d * rh, rh), :]
        return rcopy(ref, ref, p1_s.at[arr, d, s], p1_r.at[arr, d, s], (y_to, x_to)[arr][d])

    def p2_ref(arr, d, blk):
        if arr == 0:
            return tok.at[blk, c, pl.ds(d * bh, bh), :]
        return grd.at[:, c, sized(blk * r + d * rh, rh), :]

    def p2_copy(arr, d, s, shift):
        pos, n = ((x, nx), (y, ny))[arr]
        ref = p2_ref(arr, d, back(pos + shift, n, d, s))
        return rcopy(ref, ref, p2_s.at[arr, d, s], p2_r.at[arr, d, s], (x_to, y_to)[arr][d])

    def shift_of(d):
        return -1 if d == 0 else 1

    p1_n, p2_n = (ny - 1, nx - 1), (nx - 1, ny - 1)
    def pc_copy(arr, idx, core):
        if idx == 0:
            ref = tok.at[x, core] if arr == 0 else grd.at[:, core, sized(y * r, r), :]
        else:
            s, d = (idx - 1) // 2, (idx - 1) % 2
            pos, n = ((x, nx), (y, ny))[arr]
            blk = back(pos + shift_of(d), n, d, s)
            ref = tok.at[blk, core, pl.ds(d * bh, bh), :] if arr == 0 else grd.at[:, core, sized(blk * r + d * rh, rh), :]
        return rcopy(ref, ref, pc_s.at[arr, idx], pc_r.at[arr, idx], mate)

    def p1_event(s):
        for arr in (0, 1):
            for d in (0, 1):
                if 0 < s <= p1_n[arr]:
                    p1_copy(arr, d, s - 1, shift_of(d)).wait_recv()
                if s < p1_n[arr]:
                    p1_copy(arr, d, s, 0).start()

    def p2_event(s):
        for arr in (0, 1):
            for d in (0, 1):
                if 0 < s <= p2_n[arr]:
                    p2_copy(arr, d, s - 1, shift_of(d)).wait_recv()
                if s < p2_n[arr]:
                    p2_copy(arr, d, s, 0).start()
                if 0 < s <= p2_n[arr]:
                    pc_copy(arr, 1 + 2 * (s - 1) + d, c).start()
            if s == 0:
                pc_copy(arr, 0, c).start()

    def z_event(s):
        for m in range(3):
            for d in (0, 1):
                if s > 0:
                    ag_wait(m, d, s - 1)
                if s < nz - 1:
                    ag_send(m, d, s)

    for k in range(1, nd):
        a2a(0, k).start()
    for cp in loads:
        cp.wait()
    p1_event(0)
    for m in (1, 2):
        for k in range(1, nd):
            a2a(m, k).start()
    p1_event(1)
    for m in range(3):
        for k in range(1, nd):
            a2a_wait(m, k)
        for d in (0, 1):
            ag_send(m, d, 0)
    p1_last, p2_last = max(p1_n), max(p2_n)
    for s in range(2, p1_last + 1):
        p1_event(s)
    p2_at = {0: 0.0}
    for s in range(1, p2_last + 1):
        p2_at[s] = s * 11.5
    marks = [(p2_at[s], 0, s) for s in p2_at] + [(4.0 + 8.2 * (s - 1), 1, s) for s in range(1, nz)]
    for _, kind, s in sorted(marks):
        (p2_event, z_event)[kind](s)
    for arr in (0, 1):
        for idx in range(1 + 2 * p2_n[arr]):
            pc_copy(arr, idx, 1 - c).wait_recv()

    def act_block(t, carry):
        i, half = t // 2, lax.rem(t, 2)
        sl = sized(half * hf, hf)
        xi, ci = i // CORES, lax.rem(i, CORES)
        x_rows, g_rows = tok[xi, ci], grd[xi, ci]
        gate_pre = dot(x_rows, wgt[0, :, sl], 1, 0).astype(BF).astype(F32)
        up_pre = dot(x_rows, wgt[1, :, sl], 1, 0).astype(BF).astype(F32)
        grad_h = dot(g_rows, wgt[2, :, sl], 1, 0).astype(BF).astype(F32)
        sig = jax.nn.sigmoid(gate_pre)
        silu = gate_pre * sig
        vals = ((grad_h * up_pre * sig * (1.0 + gate_pre * (1.0 - sig))).astype(BF), (grad_h * silu).astype(BF), (silu * up_pre).astype(BF))
        for m in range(3):
            act[m, i, :, sl] = vals[m]
            act_t[m, sl, sized(i * br, br)] = vals[m].T
        return carry

    lax.fori_loop(0, nd * 2, act_block, 0)

    outs = (dg_ref, du_ref, dd_ref)

    def part(m, d, blk):
        src = grd if m == 2 else tok
        rhs = src[:, :, :, sized(blk * zb, zb)].reshape(nd * br, zb)
        return dot(act_t[m, pl.ds(d * hf, hf), :], rhs, 1, 0)

    def rs_copy(m, d, s):
        slot = lax.rem(s, 2)
        return rcopy(zsend.at[m, d, slot], zrecv.at[m, d, slot], rs_s.at[m, d, s], rs_r.at[m, d, s], z_to[d])

    def rs_step(s, first):
        for m in range(3):
            for d in (0, 1):
                blk = lax.rem(z - 1 - s + 2 * nz, nz) if d == 0 else lax.rem(z + 1 + s, nz)
                val = part(m, d, blk)
                if not first:
                    rs_copy(m, d, s - 1).wait_recv()
                    val = val + zrecv[m, d, lax.rem(s - 1, 2)]

                    @pl.when(s >= 2)
                    def _():
                        rs_copy(m, d, s - 2).wait_send()

                zsend[m, d, lax.rem(s, 2)] = val
                if not first:

                    @pl.when(s <= nz - 3)
                    def _():
                        pl.semaphore_signal(credit.at[m, d], inc=1, device_id=z_to[1 - d], device_id_type=pl.DeviceIdType.MESH)

                    @pl.when(s >= 2)
                    def _():
                        pl.semaphore_wait(credit.at[m, d], 1)

                rs_copy(m, d, s).start()

    rs_step(0, True)

    cols = d_model // 4

    def ex_copy(arr, xi):
        return rcopy(stage.at[arr], ysum.at[arr, xi], ex_s.at[arr, xi], ex_r.at[arr, xi], mate)

    def row_part(arr, i, j):
        sl = sized(j * cols, cols)
        if arr == 0:
            return dot(act[2, i], wgt[2, sl, :], 1, 1)
        return dot(act[0, i], wgt[0, sl, :], 1, 1) + dot(act[1, i], wgt[1, sl, :], 1, 1)

    def give(xi, carry):
        for arr in (0, 1):

            @pl.when(xi >= 1)
            def _():
                ex_copy(arr, xi - 1).wait_send()

            def fill(j, carry):
                stage[arr, :, sized(j * cols, cols)] = row_part(arr, xi * CORES + 1 - c, j).astype(BF)
                return carry

            lax.fori_loop(0, d_model // cols, fill, 0)
            ex_copy(arr, xi).start()
        return carry

    lax.fori_loop(0, nx, give, 0)

    def keep(xi, carry):
        for arr in (0, 1):
            ex_copy(arr, xi).wait_recv()

            def fill(j, carry):
                sl = sized(j * cols, cols)
                mine = row_part(arr, xi * CORES + c, j).astype(BF).astype(F32)
                ysum[arr, xi, :, sl] = (mine + ysum[arr, xi, :, sl].astype(F32)).astype(BF)
                return carry

            lax.fori_loop(0, d_model // cols, fill, 0)
        return carry

    lax.fori_loop(0, nx, keep, 0)

    sa_n, sb_n = (nx - 1, ny - 1), (ny - 1, nx - 1)
    recv_a, recv_b = (ya_recv, xa_recv), (yb_recv, xb_recv)

    def sa_ref(arr, d, blk):
        if arr == 0:
            return ysum.at[0, blk, pl.ds(d * bh, bh), :]
        return ysum.at[1, :, sized(blk * r + d * rh, rh), :]

    def sb_ref(arr, d, blk):
        if arr == 0:
            return ysum.at[0, x, sized(blk * r + d * rh, rh), :]
        return ysum.at[1, blk, sized(y * r + d * rh, rh), :]

    def add_into(ref, slot):
        flat = len(ref.shape) == 2
        count = ref.shape[0] // 16 if flat else ref.shape[0]

        def piece(i, carry):
            at = sized(i * 16, 16) if flat else i
            ref[at] = (ref[at].astype(F32) + slot[at].astype(F32)).astype(BF)
            return carry

        lax.fori_loop(0, count, piece, 0)

    def scatter_event(refs, counts, recv, ss, rr, to, pos, s, last):
        for arr in (0, 1):
            n = counts[arr] + 1
            if s > counts[arr]:
                continue
            for d in (0, 1):
                blk = back(pos[arr] + shift_of(d), n, d, s)
                ref = refs(arr, d, blk)
                if s > 0:
                    slot = recv[arr].at[d, s - 1]
                    rcopy(slot, slot, ss.at[arr, d, s - 1], rr.at[arr, d, s - 1], to[arr][d]).wait_recv()
                    add_into(ref, slot)
                if s < counts[arr]:
                    rcopy(ref, recv[arr].at[d, s], ss.at[arr, d, s], rr.at[arr, d, s], to[arr][d]).start()

    def sa_event(s):
        scatter_event(sa_ref, sa_n, recv_a, sa_s, sa_r, (x_to, y_to), (x, y), s, False)

    def sb_event(s):
        scatter_event(sb_ref, sb_n, recv_b, sb_s, sb_r, (y_to, x_to), (y, x), s, True)

    def sb_finish():
        for arr, dst in ((0, out_ref), (1, gin_ref)):
            total = ysum[arr, x, sized(y * r, r), :].astype(F32)
            dst[...] = (own[arr][...].astype(F32) + total).astype(BF)

    sa_event(0)
    steps = [[functools.partial(sa_event, s)] for s in range(1, max(sa_n) + 1)]
    steps[-1].append(functools.partial(sb_event, 0))
    steps += [[functools.partial(sb_event, s)] for s in range(1, max(sb_n) + 1)]
    steps[-1].append(sb_finish)

    def ring(s, carry):
        rs_step(s, False)
        for k, fs in enumerate(steps[: nz - 2]):

            @pl.when(s == k + 1)
            def _(fs=fs):
                for f in fs:
                    f()

        return carry

    lax.fori_loop(1, nz - 1, ring, 0)
    for fs in steps[nz - 2:]:
        for f in fs:
            f()

    spare = (nz - 1) % 2

    def fin_copy(m, d, k):
        to = lax.rem(me + k, nd)
        return rcopy(zsend.at[m, d, spare, sized(to * dp, dp), :], outs[m].at[:, sized(me * fo + d * hf, hf)],
                     fa_s.at[m, d, k - 1], fa_r.at[m, d, k - 1], {"data": to})

    for m in range(3):
        for d in (0, 1):
            val = part(m, d, z)
            rs_copy(m, d, nz - 2).wait_recv()
            rs_copy(m, d, nz - 3).wait_send()
            zsend[m, d, spare] = (val + zrecv[m, d, nz % 2]).T
            for k in range(1, nd):
                fin_copy(m, d, k).start()
            outs[m][:, sized(me * fo + d * hf, hf)] = zsend[m, d, spare, sized(me * dp, dp), :]

    for m in range(3):
        for k in range(1, nd):
            frm = lax.rem(me + nd - k, nd)
            for d in (0, 1):
                dst = outs[m].at[:, sized(frm * fo + d * hf, hf)]
                rcopy(dst, dst, fa_s.at[m, d, k - 1], fa_r.at[m, d, k - 1], {"data": frm}).wait_recv()
                fin_copy(m, d, k).wait_send()
            a2a(m, k).wait_send()
        for d in (0, 1):
            for s in range(nz - 1):
                ag_copy(m, d, s, z).wait_send()
            rs_copy(m, d, nz - 2).wait_send()
    for arr in (0, 1):
        for d in (0, 1):
            for s in range(p1_n[arr]):
                p1_copy(arr, d, s, 0).wait_send()
            for s in range(p2_n[arr]):
                p2_copy(arr, d, s, 0).wait_send()
            for s in range(sa_n[arr]):
                ref = recv_a[arr].at[d, s]
                rcopy(ref, ref, sa_s.at[arr, d, s], sa_r.at[arr, d, s], z_to[0]).wait_send()
            for s in range(sb_n[arr]):
                ref = recv_b[arr].at[d, s]
                rcopy(ref, ref, sb_s.at[arr, d, s], sb_r.at[arr, d, s], z_to[0]).wait_send()
        for idx in range(1 + 2 * p2_n[arr]):
            pc_copy(arr, idx, c).wait_send()
        ex_copy(arr, nx - 1).wait_send()


def solution(mesh):
    nz, ny, nd = mesh.shape["datb"], mesh.shape["model"], mesh.shape["data"]
    nx = nd // CORES

    def local_step(tok_loc, wg_loc, wu_loc, wd_loc, grad_loc):
        r, d_model = tok_loc.shape
        dp, fp = wg_loc.shape
        fo = fp // nd
        hf, zb, br = fo // 2, dp * nd, r * ny
        bh, rh = br // 2, r // 2
        vmem = pl.BlockSpec(memory_space=pltpu.VMEM)
        hbm = pl.BlockSpec(memory_space=pl.ANY)
        dma = pltpu.SemaphoreType.DMA
        most = max(nx, ny) - 1
        out, gin, dg, du, dd = pl.pallas_call(
            functools.partial(kernel, nz, ny, nx),
            out_shape=[jax.ShapeDtypeStruct((r, d_model), BF)] * 2 + [jax.ShapeDtypeStruct((dp, fp), F32)] * 3,
            in_specs=[hbm] * 5,
            out_specs=[vmem] * 5,
            scratch_shapes=[
                pltpu.VMEM((nx, CORES, br, d_model), BF),
                pltpu.VMEM((nx, CORES, br, d_model), BF),
                pltpu.VMEM((3, d_model, fo), BF),
                pltpu.VMEM((3, nd, br, fo), BF),
                pltpu.VMEM((3, fo, nd * br), BF),
                pltpu.VMEM((3, 2, 2, hf, zb), F32),
                pltpu.VMEM((3, 2, 2, hf, zb), F32),
                pltpu.VMEM((2, nx, br, d_model), BF),
                pltpu.VMEM((2, br, d_model), BF),
                pltpu.VMEM((2, nx - 1, bh, d_model), BF),
                pltpu.VMEM((2, ny - 1, nx, rh, d_model), BF),
                pltpu.VMEM((2, ny - 1, rh, d_model), BF),
                pltpu.VMEM((2, nx - 1, rh, d_model), BF),
                dma((5,)),
                dma((3, nd - 1)), dma((3, nd - 1)),
                dma((3, 2, nz - 1)), dma((3, 2, nz - 1)),
                dma((2, 2, most)), dma((2, 2, most)),
                dma((2, 2, most)), dma((2, 2, most)),
                dma((2, 1 + 2 * most)), dma((2, 1 + 2 * most)),
                dma((3, 2, nz - 1)), dma((3, 2, nz - 1)),
                pltpu.SemaphoreType.REGULAR((3, 2)),
                dma((2, nx)), dma((2, nx)),
                dma((2, 2, most)), dma((2, 2, most)),
                dma((2, 2, most)), dma((2, 2, most)),
                dma((3, 2, nd - 1)), dma((3, 2, nd - 1)),
            ],
            compiler_params=pltpu.CompilerParams(collective_id=0, has_side_effects=True, vmem_limit_bytes=67043328),
            name="swiglu_step",
        )(tok_loc, grad_loc, wg_loc, wu_loc, wd_loc.T)
        return out, gin, dg, du, dd.T

    return jax.shard_map(local_step, mesh=mesh, in_specs=(ROW_SPEC, GATE_SPEC, GATE_SPEC, DOWN_SPEC, ROW_SPEC), out_specs=(ROW_SPEC, ROW_SPEC, GATE_SPEC, GATE_SPEC, DOWN_SPEC), check_vma=False)
```

time: 668 us -> 262 us (0.39); the launches traced: 657 us -> 262 us
  waiting for transfers between devices: 483 us -> 0 us
  Pallas kernels: 0 us -> 256 us
  matrix products: 100 us -> 0 us
  starting transfers between devices: 20.4 us -> 0 us
  blocking collectives: 17.7 us -> 0 us
  between operations: 14.5 us -> 0.66 us
  local copies, waits for them, and re-layouts: 17.1 us -> 5.7 us
    reduce_scatter x5 -> x0, waiting for transfers between devices: 266 us -> none  [the longest x1 102 us: local_step(): lax.psum_scatter(back_part, ('data', 'model'), scatter_dimension=0, tiled...]
    pallas_call x0 -> x1, Pallas kernels: none -> 256 us  [local_step(): pl.pallas_call(functools.partial(kernel, nz, ny, nx), out_shape=[jax.Shap...]
    all_gather x5 -> x0, waiting for transfers between devices: 208 us -> none  [the longest x1 63.2 us: local_step(): tok = lax.all_gather(tok_loc, ('data', 'model'), axis=0, tiled=True)]
    dot_general x9 -> x0, matrix products: 100 us -> none  [dot(): lax.dot_general(lhs, rhs, (((ldim,), (rdim,)), ((), ())), preferred_eleme...]
    all_to_all x3 -> x0, starting transfers between devices: 19.8 us -> none  [home(): lax.all_to_all(moved, 'data', 0, 1, tiled=False).reshape(d_part, f_part)]
    all_to_all x1 -> x0, blocking collectives: 17.7 us -> none  [local_step(): mine = lax.all_to_all(mine, 'data', 2, 1, tiled=False)]
    all_to_all x3 -> x0, waiting for transfers between devices: 7.48 us -> none  [home(): lax.all_to_all(moved, 'data', 0, 1, tiled=False).reshape(d_part, f_part)]
  transfers between devices with their start and end apart: 13 -> 0, of which waited for: 10 -> 0; matrix products, arithmetic and copies ran while one was open for 17% -> 0% of each run, Pallas kernels for 0% -> 0%
where the time goes in v2:
time: 262 us
  Pallas kernels  256 us (98%)
  local copies, waits for them, and re-layouts  5.7 us (2%)
    pallas_call x1, Pallas kernels, local_step(): pl.pallas_call(functools.partial(kernel, nz, ny, nx), out_shape=[jax.Shap...  256 us
    unnamed x13, local copies, waits for them, and re-layouts  5.7 us

profile of v2, /device:TPU:1, one launch (start us, length us, event | category | flops | bytes accessed | tf_op | source)
XLA Modules:
  0.0 262.0 jit_solution(6307125989931110659)
XLA Ops:
  0.6 255.6 %swiglu_step.1 = (bf16[64,2048]{1,0:T(8,128)(2,1)}, bf16[64,2048]{1,0:T(8,128)(2,1)}, f32[32,4096]{1,0:T(8,128)}, f32[32,4096]{1,0:T(8,128)}, f32[32,4096]{1,0:T(8,128)}) custom-call(bf16[64,2048]{1,0:T(8,128)(2,1)} %tok_in.1, bf16[64,2048]{1,0:T(8,128)(2,1)} %grad_in.1, bf16[32,4096]{1,0:T(8,128)(2,1)} %wg_in.1, bf16[32,4096]{1,0:T(8,128)(2,1)} %wu_in.1, ...), custom_call_target="tpu_custom_call" | custom-call | tf_op jit(solution)/shard_map/swiglu_step/pallas_call | solution.py:404
  256.3 0.0 copy-start.3
  256.3 0.0 copy-start.2
  256.3 1.7 copy.15
  258.0 0.0 copy-done.3
  258.0 0.7 copy.16
  258.7 0.0 copy-done.2
  258.7 0.0 copy-start.1
  258.7 0.8 copy.17
  259.5 0.4 copy-done.1
  260.0 0.0 copy-start
  260.0 0.8 copy.18
  260.8 0.4 copy-done
  261.2 0.8 copy.19
Async XLA Ops:
  256.3 1.8 copy-start.3
  256.3 2.5 copy-start.2
  258.7 1.2 copy-start.1
  260.0 1.2 copy-start

commit v3 on v2

--- a/solution.py
+++ b/solution.py
@@ -71,121 +71,125 @@
         dst = wgt.at[m, sized(z * zb + frm * dp, dp), :]
         rcopy(dst, dst, a2a_s.at[m, k - 1], a2a_r.at[m, k - 1], {"data": frm}).wait_recv()
 
-    def ag_copy(m, d, s, pos):
-        ref = wgt.at[m, sized(back(pos, nz, d, s) * zb, zb), pl.ds(d * hf, hf)]
-        return rcopy(ref, ref, ag_s.at[m, d, s], ag_r.at[m, d, s], z_to[d])
-
-    def ag_send(m, d, s):
-        ag_copy(m, d, s, z).start()
-
-    def ag_wait(m, d, s):
-        ag_copy(m, d, s, z - 1 if d == 0 else z + 1).wait_recv()
-
-    def p1_copy(arr, d, s, shift):
+    streams = ((0, 0, zb), (1, 0, zb), (2, 0, zb // 2), (2, zb // 2, zb // 2))
+
+    def ag_copy(q, d, s, ahead):
+        m, first, rows = streams[q]
+        ref = wgt.at[m, sized(back(z, nz, d, s + ahead) * zb + first, rows), pl.ds(d * hf, hf)]
+        return rcopy(ref, ref, ag_s.at[q, d, s], ag_r.at[q, d, s], z_to[d])
+
+    def z_event(m, s):
+        for q in range(4):
+            if streams[q][0] == m:
+                for d in (0, 1):
+                    if s > 0:
+                        ag_copy(q, d, s - 1, 1).wait_recv()
+                    if s < nz - 1:
+                        ag_copy(q, d, s, 0).start()
+
+    first_n, second_n = (ny, nx), (nx, ny)
+    first_to, second_to = (y_to, x_to), (x_to, y_to)
+
+    def cell(arr, j, t, h, core):
         if arr == 0:
-            pos = y + shift
-            ref = tok.at[x, c, sized(back(pos, ny, d, s) * r + d * rh, rh), :]
-        else:
-            pos = x + shift
-            ref = grd.at[back(pos, nx, d, s), c, sized(y * r + d * rh, rh), :]
-        return rcopy(ref, ref, p1_s.at[arr, d, s], p1_r.at[arr, d, s], (y_to, x_to)[arr][d])
-
-    def p2_ref(arr, d, blk):
-        if arr == 0:
-            return tok.at[blk, c, pl.ds(d * bh, bh), :]
-        return grd.at[:, c, sized(blk * r + d * rh, rh), :]
-
-    def p2_copy(arr, d, s, shift):
-        pos, n = ((x, nx), (y, ny))[arr]
-        ref = p2_ref(arr, d, back(pos + shift, n, d, s))
-        return rcopy(ref, ref, p2_s.at[arr, d, s], p2_r.at[arr, d, s], (x_to, y_to)[arr][d])
-
-    def shift_of(d):
-        return -1 if d == 0 else 1
-
-    p1_n, p2_n = (ny - 1, nx - 1), (nx - 1, ny - 1)
-    def pc_copy(arr, idx, core):
-        if idx == 0:
-            ref = tok.at[x, core] if arr == 0 else grd.at[:, core, sized(y * r, r), :]
-        else:
-            s, d = (idx - 1) // 2, (idx - 1) % 2
-            pos, n = ((x, nx), (y, ny))[arr]
-            blk = back(pos + shift_of(d), n, d, s)
-            ref = tok.at[blk, core, pl.ds(d * bh, bh), :] if arr == 0 else grd.at[:, core, sized(blk * r + d * rh, rh), :]
-        return rcopy(ref, ref, pc_s.at[arr, idx], pc_r.at[arr, idx], mate)
-
-    def p1_event(s):
+            return tok.at[back(x, nx, h, t), core, sized(back(y, ny, h, j) * r + h * rh, rh), :]
+        return grd.at[back(x, nx, h, j), core, sized(back(y, ny, h, t) * r + h * rh, rh), :]
+
+    def p1_copy(arr, h, j, ahead):
+        ref = cell(arr, j + ahead, 0, h, c)
+        return rcopy(ref, ref, p1_s.at[arr, h, j], p1_r.at[arr, h, j], first_to[arr][h])
+
+    def p2_copy(arr, h, j, t, ahead):
+        ref = cell(arr, j, t + ahead, h, c)
+        return rcopy(ref, ref, p2_s.at[arr, h, j, t], p2_r.at[arr, h, j, t], second_to[arr][h])
+
+    def pc_copy(arr, h, j, t, core):
+        ref = cell(arr, j, t, h, core)
+        return rcopy(ref, ref, pc_s.at[arr, h, j, t], pc_r.at[arr, h, j, t], mate)
+
+    def token_event(j, t):
         for arr in (0, 1):
-            for d in (0, 1):
-                if 0 < s <= p1_n[arr]:
-                    p1_copy(arr, d, s - 1, shift_of(d)).wait_recv()
-                if s < p1_n[arr]:
-                    p1_copy(arr, d, s, 0).start()
-
-    def p2_event(s):
-        for arr in (0, 1):
-            for d in (0, 1):
-                if 0 < s <= p2_n[arr]:
-                    p2_copy(arr, d, s - 1, shift_of(d)).wait_recv()
-                if s < p2_n[arr]:
-                    p2_copy(arr, d, s, 0).start()
-                if 0 < s <= p2_n[arr]:
-                    pc_copy(arr, 1 + 2 * (s - 1) + d, c).start()
-            if s == 0:
-                pc_copy(arr, 0, c).start()
-
-    def z_event(s):
-        for m in range(3):
-            for d in (0, 1):
-                if s > 0:
-                    ag_wait(m, d, s - 1)
-                if s < nz - 1:
-                    ag_send(m, d, s)
-
-    for k in range(1, nd):
-        a2a(0, k).start()
+            if j < first_n[arr] and t < second_n[arr]:
+                for h in (0, 1):
+                    if t > 0:
+                        p2_copy(arr, h, j, t - 1, 1).wait_recv()
+                    elif j > 0:
+                        p1_copy(arr, h, j - 1, 1).wait_recv()
+                    if t == 0 and j < first_n[arr] - 1:
+                        p1_copy(arr, h, j, 0).start()
+                    if t < second_n[arr] - 1:
+                        p2_copy(arr, h, j, t, 0).start()
+                    pc_copy(arr, h, j, t, c).start()
+
+    def a2a_event(m):
+        for k in range(1, nd):
+            a2a_wait(m, k)
+        z_event(m, 0)
+
+    for m in range(3):
+        for k in range(1, nd):
+            a2a(m, k).start()
     for cp in loads:
         cp.wait()
-    p1_event(0)
-    for m in (1, 2):
-        for k in range(1, nd):
-            a2a(m, k).start()
-    p1_event(1)
+
+    most = max(nx, ny)
+    marks = []
+    sends = 0
+    for ready, j, t in sorted((4.2 * j + 5.4 * t, j, t) for j in range(most) for t in range(most)):
+        marks.append((10.0 * (j + t > 0) + max(ready, 3.4 * sends), len(marks), functools.partial(token_event, j, t)))
+        sends += t < most - 1
     for m in range(3):
-        for k in range(1, nd):
-            a2a_wait(m, k)
-        for d in (0, 1):
-            ag_send(m, d, 0)
-    p1_last, p2_last = max(p1_n), max(p2_n)
-    for s in range(2, p1_last + 1):
-        p1_event(s)
-    p2_at = {0: 0.0}
-    for s in range(1, p2_last + 1):
-        p2_at[s] = s * 11.5
-    marks = [(p2_at[s], 0, s) for s in p2_at] + [(4.0 + 8.2 * (s - 1), 1, s) for s in range(1, nz)]
-    for _, kind, s in sorted(marks):
-        (p2_event, z_event)[kind](s)
+        marks.append((5.0 + 2.0 * m, len(marks), functools.partial(a2a_event, m)))
+    ring_order = [(m, s) for s in range(1, nz) for m in (0, 1, 2)[: 3 if s % 2 == 0 else 2]]
+    ring_order = [(m, s if m < 2 else s // 2) for m, s in ring_order]
+    clock = 12.0
+    for m, s in ring_order:
+        marks.append((clock, len(marks), functools.partial(z_event, m, s)))
+        clock += 2.8
+    for _, _, f in sorted(marks, key=lambda mark: mark[:2]):
+        f()
+    late = [s for s in range(1, nz) if (2, s) not in ring_order]
     for arr in (0, 1):
-        for idx in range(1 + 2 * p2_n[arr]):
-            pc_copy(arr, idx, 1 - c).wait_recv()
-
-    def act_block(t, carry):
+        for h in (0, 1):
+            for j in range(first_n[arr]):
+                for t in range(second_n[arr]):
+                    pc_copy(arr, h, j, t, 1 - c).wait_recv()
+
+    def blocks(t):
         i, half = t // 2, lax.rem(t, 2)
-        sl = sized(half * hf, hf)
-        xi, ci = i // CORES, lax.rem(i, CORES)
-        x_rows, g_rows = tok[xi, ci], grd[xi, ci]
-        gate_pre = dot(x_rows, wgt[0, :, sl], 1, 0).astype(BF).astype(F32)
-        up_pre = dot(x_rows, wgt[1, :, sl], 1, 0).astype(BF).astype(F32)
-        grad_h = dot(g_rows, wgt[2, :, sl], 1, 0).astype(BF).astype(F32)
+        return i, i // CORES, lax.rem(i, CORES), sized(half * hf, hf)
+
+    def forward_block(t, carry):
+        i, xi, ci, sl = blocks(t)
+        x_rows = tok[xi, ci]
+        gate_b = dot(x_rows, wgt[0, :, sl], 1, 0).astype(BF)
+        up_b = dot(x_rows, wgt[1, :, sl], 1, 0).astype(BF)
+        gate_pre, up_pre = gate_b.astype(F32), up_b.astype(F32)
+        hidden = (gate_pre * jax.nn.sigmoid(gate_pre) * up_pre).astype(BF)
+        act[0, i, :, sl] = gate_b
+        act[1, i, :, sl] = up_b
+        act[2, i, :, sl] = hidden
+        act_t[2, sl, sized(i * br, br)] = hidden.T
+        for n, s in enumerate(late):
+
+            @pl.when(t == (n + 1) * 2 * nd // len(late) - 1)
+            def _():
+                z_event(2, s)
+
+        return carry
+
+    lax.fori_loop(0, nd * 2, forward_block, 0)
+
+    def backward_block(t, carry):
+        i, xi, ci, sl = blocks(t)
+        gate_pre, up_pre = act[0, i, :, sl].astype(F32), act[1, i, :, sl].astype(F32)
+        grad_h = dot(grd[xi, ci], wgt[2, :, sl], 1, 0).astype(BF).astype(F32)
         sig = jax.nn.sigmoid(gate_pre)
-        silu = gate_pre * sig
-        vals = ((grad_h * up_pre * sig * (1.0 + gate_pre * (1.0 - sig))).astype(BF), (grad_h * silu).astype(BF), (silu * up_pre).astype(BF))
-        for m in range(3):
+        vals = ((grad_h * up_pre * sig * (1.0 + gate_pre * (1.0 - sig))).astype(BF), (grad_h * (gate_pre * sig)).astype(BF))
+        for m in range(2):
             act[m, i, :, sl] = vals[m]
             act_t[m, sl, sized(i * br, br)] = vals[m].T
         return carry
-
-    lax.fori_loop(0, nd * 2, act_block, 0)
 
     outs = (dg_ref, du_ref, dd_ref)
 
@@ -198,33 +202,37 @@
         slot = lax.rem(s, 2)
         return rcopy(zsend.at[m, d, slot], zrecv.at[m, d, slot], rs_s.at[m, d, s], rs_r.at[m, d, s], z_to[d])
 
-    def rs_step(s, first):
-        for m in range(3):
-            for d in (0, 1):
-                blk = lax.rem(z - 1 - s + 2 * nz, nz) if d == 0 else lax.rem(z + 1 + s, nz)
-                val = part(m, d, blk)
-                if not first:
-                    rs_copy(m, d, s - 1).wait_recv()
-                    val = val + zrecv[m, d, lax.rem(s - 1, 2)]
-
-                    @pl.when(s >= 2)
-                    def _():
-                        rs_copy(m, d, s - 2).wait_send()
-
-                zsend[m, d, lax.rem(s, 2)] = val
-                if not first:
-
-                    @pl.when(s <= nz - 3)
-                    def _():
-                        pl.semaphore_signal(credit.at[m, d], inc=1, device_id=z_to[1 - d], device_id_type=pl.DeviceIdType.MESH)
-
-                    @pl.when(s >= 2)
-                    def _():
-                        pl.semaphore_wait(credit.at[m, d], 1)
-
-                rs_copy(m, d, s).start()
-
-    rs_step(0, True)
+    def shift_of(d):
+        return -1 if d == 0 else 1
+
+    def rs_chunk(m, s, first):
+        for d in (0, 1):
+            blk = lax.rem(z - 1 - s + 2 * nz, nz) if d == 0 else lax.rem(z + 1 + s, nz)
+            val = part(m, d, blk)
+            if not first:
+                rs_copy(m, d, s - 1).wait_recv()
+                val = val + zrecv[m, d, lax.rem(s - 1, 2)]
+
+                @pl.when(s >= 2)
+                def _():
+                    rs_copy(m, d, s - 2).wait_send()
+
+            zsend[m, d, lax.rem(s, 2)] = val
+            if not first:
+
+                @pl.when(s <= nz - 3)
+                def _():
+                    pl.semaphore_signal(credit.at[m, d], inc=1, device_id=z_to[1 - d], device_id_type=pl.DeviceIdType.MESH)
+
+                @pl.when(s >= 2)
+                def _():
+                    pl.semaphore_wait(credit.at[m, d], 1)
+
+            rs_copy(m, d, s).start()
+
+    order = (2, 0, 1)
+    rs_chunk(2, 0, True)
+    lax.fori_loop(0, nd * 2, backward_block, 0)
 
     cols = d_model // 4
 
@@ -237,11 +245,9 @@
             return dot(act[2, i], wgt[2, sl, :], 1, 1)
         return dot(act[0, i], wgt[0, sl, :], 1, 1) + dot(act[1, i], wgt[1, sl, :], 1, 1)
 
-    def give(xi, carry):
+    def give(xi):
         for arr in (0, 1):
-
-            @pl.when(xi >= 1)
-            def _():
+            if xi >= 1:
                 ex_copy(arr, xi - 1).wait_send()
 
             def fill(j, carry):
@@ -250,11 +256,8 @@
 
             lax.fori_loop(0, d_model // cols, fill, 0)
             ex_copy(arr, xi).start()
-        return carry
-
-    lax.fori_loop(0, nx, give, 0)
-
-    def keep(xi, carry):
+
+    def keep(xi):
         for arr in (0, 1):
             ex_copy(arr, xi).wait_recv()
 
@@ -265,9 +268,6 @@
                 return carry
 
             lax.fori_loop(0, d_model // cols, fill, 0)
-        return carry
-
-    lax.fori_loop(0, nx, keep, 0)
 
     sa_n, sb_n = (nx - 1, ny - 1), (ny - 1, nx - 1)
     recv_a, recv_b = (ya_recv, xa_recv), (yb_recv, xb_recv)
@@ -319,26 +319,40 @@
             total = ysum[arr, x, sized(y * r, r), :].astype(F32)
             dst[...] = (own[arr][...].astype(F32) + total).astype(BF)
 
-    sa_event(0)
-    steps = [[functools.partial(sa_event, s)] for s in range(1, max(sa_n) + 1)]
-    steps[-1].append(functools.partial(sb_event, 0))
-    steps += [[functools.partial(sb_event, s)] for s in range(1, max(sb_n) + 1)]
-    steps[-1].append(sb_finish)
+    slots = 3 * (nz - 1)
+    work = [functools.partial(give, xi) for xi in range(nx)] + [functools.partial(keep, xi) for xi in range(nx)]
+    plan = list(enumerate(work, 1))
+    at = 1 + len(work)
+    for s in range(max(sa_n) + 1):
+        plan.append((at + 3 * s, functools.partial(sa_event, s)))
+    at += 3 * max(sa_n)
+    for s in range(max(sb_n) + 1):
+        plan.append((at + s, functools.partial(sb_event, s)))
+    plan.append((at + max(sb_n), sb_finish))
+
+    for idx in (1, 2):
+        rs_chunk(order[idx], 0, True)
+        for slot, f in plan:
+            if slot == idx:
+                f()
 
     def ring(s, carry):
-        rs_step(s, False)
-        for k, fs in enumerate(steps[: nz - 2]):
-
-            @pl.when(s == k + 1)
-            def _(fs=fs):
-                for f in fs:
-                    f()
+        for idx, m in enumerate(order):
+            rs_chunk(m, s, False)
+            for k in range(1, nz - 1):
+                fs = [f for slot, f in plan if slot == 3 * k + idx]
+                if fs:
+
+                    @pl.when(s == k)
+                    def _():
+                        for f in fs:
+                            f()
 
         return carry
 
     lax.fori_loop(1, nz - 1, ring, 0)
-    for fs in steps[nz - 2:]:
-        for f in fs:
+    for slot, f in plan:
+        if slot >= slots:
             f()
 
     spare = (nz - 1) % 2
@@ -348,7 +362,7 @@
         return rcopy(zsend.at[m, d, spare, sized(to * dp, dp), :], outs[m].at[:, sized(me * fo + d * hf, hf)],
                      fa_s.at[m, d, k - 1], fa_r.at[m, d, k - 1], {"data": to})
 
-    for m in range(3):
+    for m in order:
         for d in (0, 1):
             val = part(m, d, z)
             rs_copy(m, d, nz - 2).wait_recv()
@@ -358,7 +372,7 @@
                 fin_copy(m, d, k).start()
             outs[m][:, sized(me * fo + d * hf, hf)] = zsend[m, d, spare, sized(me * dp, dp), :]
 
-    for m in range(3):
+    for m in order:
         for k in range(1, nd):
             frm = lax.rem(me + nd - k, nd)
             for d in (0, 1):
@@ -367,23 +381,26 @@
                 fin_copy(m, d, k).wait_send()
             a2a(m, k).wait_send()
         for d in (0, 1):
+            rs_copy(m, d, nz - 2).wait_send()
+    for q in range(4):
+        for d in (0, 1):
             for s in range(nz - 1):
-                ag_copy(m, d, s, z).wait_send()
-            rs_copy(m, d, nz - 2).wait_send()
+                ag_copy(q, d, s, 0).wait_send()
     for arr in (0, 1):
-        for d in (0, 1):
-            for s in range(p1_n[arr]):
-                p1_copy(arr, d, s, 0).wait_send()
-            for s in range(p2_n[arr]):
-                p2_copy(arr, d, s, 0).wait_send()
+        for h in (0, 1):
+            for j in range(first_n[arr]):
+                if j < first_n[arr] - 1:
+                    p1_copy(arr, h, j, 0).wait_send()
+                for t in range(second_n[arr]):
+                    if t < second_n[arr] - 1:
+                        p2_copy(arr, h, j, t, 0).wait_send()
+                    pc_copy(arr, h, j, t, c).wait_send()
             for s in range(sa_n[arr]):
-                ref = recv_a[arr].at[d, s]
-                rcopy(ref, ref, sa_s.at[arr, d, s], sa_r.at[arr, d, s], z_to[0]).wait_send()
+                ref = recv_a[arr].at[h, s]
+                rcopy(ref, ref, sa_s.at[arr, h, s], sa_r.at[arr, h, s], z_to[0]).wait_send()
             for s in range(sb_n[arr]):
-                ref = recv_b[arr].at[d, s]
-                rcopy(ref, ref, sb_s.at[arr, d, s], sb_r.at[arr, d, s], z_to[0]).wait_send()
-        for idx in range(1 + 2 * p2_n[arr]):
-            pc_copy(arr, idx, c).wait_send()
+                ref = recv_b[arr].at[h, s]
+                rcopy(ref, ref, sb_s.at[arr, h, s], sb_r.at[arr, h, s], z_to[0]).wait_send()
         ex_copy(arr, nx - 1).wait_send()
 
 
@@ -422,10 +439,10 @@
                 pltpu.VMEM((2, nx - 1, rh, d_model), BF),
                 dma((5,)),
                 dma((3, nd - 1)), dma((3, nd - 1)),
-                dma((3, 2, nz - 1)), dma((3, 2, nz - 1)),
+                dma((4, 2, nz - 1)), dma((4, 2, nz - 1)),
                 dma((2, 2, most)), dma((2, 2, most)),
-                dma((2, 2, most)), dma((2, 2, most)),
-                dma((2, 1 + 2 * most)), dma((2, 1 + 2 * most)),
+                dma((2, 2, most + 1, most)), dma((2, 2, most + 1, most)),
+                dma((2, 2, most + 1, most + 1)), dma((2, 2, most + 1, most + 1)),
                 dma((3, 2, nz - 1)), dma((3, 2, nz - 1)),
                 pltpu.SemaphoreType.REGULAR((3, 2)),
                 dma((2, nx)), dma((2, nx)),

time: 262 us -> 231 us (0.88)
  Pallas kernels: 256 us -> 225 us
    pallas_call x1, Pallas kernels: 256 us -> 225 us  [local_step(): pl.pallas_call(functools.partial(kernel, nz, ny, nx), out_shape=[jax.Shap...]
where the time goes in v3:
time: 231 us
  Pallas kernels  225 us (97%)
  local copies, waits for them, and re-layouts  5.7 us (2%)
    pallas_call x1, Pallas kernels, local_step(): pl.pallas_call(functools.partial(kernel, nz, ny, nx), out_shape=[jax.Shap...  225 us
    unnamed x13, local copies, waits for them, and re-layouts  5.7 us

profile of v3, /device:TPU:1, one launch (start us, length us, event | category | flops | bytes accessed | tf_op | source)
XLA Modules:
  0.0 231.1 jit_solution(8670729873252503854)
XLA Ops:
  0.6 224.8 %swiglu_step.1 = (bf16[64,2048]{1,0:T(8,128)(2,1)}, bf16[64,2048]{1,0:T(8,128)(2,1)}, f32[32,4096]{1,0:T(8,128)}, f32[32,4096]{1,0:T(8,128)}, f32[32,4096]{1,0:T(8,128)}) custom-call(bf16[64,2048]{1,0:T(8,128)(2,1)} %tok_in.1, bf16[64,2048]{1,0:T(8,128)(2,1)} %grad_in.1, bf16[32,4096]{1,0:T(8,128)(2,1)} %wg_in.1, bf16[32,4096]{1,0:T(8,128)(2,1)} %wu_in.1, ...), custom_call_target="tpu_custom_call" | custom-call | tf_op jit(solution)/shard_map/swiglu_step/pallas_call | solution.py:421
  225.4 0.0 copy-start.3
  225.4 0.0 copy-start.2
  225.4 1.7 copy.15
  227.2 0.0 copy-done.3
  227.2 0.7 copy.16
  227.9 0.0 copy-done.2
  227.9 0.0 copy-start.1
  227.9 0.8 copy.17
  228.7 0.4 copy-done.1
  229.1 0.0 copy-start
  229.1 0.8 copy.18
  229.9 0.4 copy-done
  230.3 0.8 copy.19
Async XLA Ops:
  225.4 1.8 copy-start.3
  225.4 2.5 %copy-start.2 = (f32[32,4096]{1,0:T(8,128)S(1)}, f32[32,4096]{1,0:T(8,128)}, u32[]{:S(2)}) copy-start(f32[32,4096]{1,0:T(8,128)} %get-tuple-element.22) | copy-start | bytes 1572868
  227.9 1.2 copy-start.1
  229.1 1.2 copy-start

commit v4 on v3

--- a/solution.py
+++ b/solution.py
@@ -26,7 +26,7 @@
 def kernel(nz, ny, nx, tok_in, grad_in, wg_in, wu_in, wd_in, out_ref, gin_ref, dg_ref, du_ref, dd_ref,
            tok, grd, wgt, act, act_t, zrecv, zsend, ysum, stage, ya_recv, xa_recv, yb_recv, xb_recv,
            in_sem, a2a_s, a2a_r, ag_s, ag_r, p1_s, p1_r, p2_s, p2_r, pc_s, pc_r, rs_s, rs_r, credit,
-           ex_s, ex_r, sa_s, sa_r, sb_s, sb_r, fa_s, fa_r):
+           ex_s, ex_r, sa_s, sa_r, sb_s, sb_r, fa_s, fa_r, fo_sem):
     z, y, me = lax.axis_index("datb"), lax.axis_index("model"), lax.axis_index("data")
     x, c = me // CORES, lax.rem(me, CORES)
     nd = nx * CORES
@@ -232,7 +232,9 @@
 
     order = (2, 0, 1)
     rs_chunk(2, 0, True)
-    lax.fori_loop(0, nd * 2, backward_block, 0)
+    lax.fori_loop(0, nd, backward_block, 0)
+    rs_chunk(2, 1, False)
+    lax.fori_loop(nd, nd * 2, backward_block, 0)
 
     cols = d_model // 4
 
@@ -319,6 +321,30 @@
             total = ysum[arr, x, sized(y * r, r), :].astype(F32)
             dst[...] = (own[arr][...].astype(F32) + total).astype(BF)
 
+    spare = (nz - 1) % 2
+    far = sorted(((g, e) for g in range(nx) for e in range(CORES) if g + e > 0), key=lambda ge: (-min(ge[0], nx - ge[0]), ge))
+
+    def place(g, e):
+        return lax.rem(x + g, nx) * CORES + (c if e == 0 else 1 - c)
+
+    def fin_copy(m, d, g, e):
+        to = place(g, e)
+        return rcopy(zsend.at[m, d, spare, sized(to * dp, dp), :], outs[m].at[:, sized(me * fo + d * hf, hf)],
+                     fa_s.at[m, d, g, e], fa_r.at[m, d, g, e], {"data": to})
+
+    def fin_own(m, d):
+        return pltpu.make_async_copy(zsend.at[m, d, spare, sized(me * dp, dp), :], outs[m].at[:, sized(me * fo + d * hf, hf)], fo_sem.at[m, d])
+
+    def finish(m):
+        for d in (0, 1):
+            val = part(m, d, z)
+            rs_copy(m, d, nz - 2).wait_recv()
+            rs_copy(m, d, nz - 3).wait_send()
+            zsend[m, d, spare] = (val + zrecv[m, d, nz % 2]).T
+            for g, e in far:
+                fin_copy(m, d, g, e).start()
+            fin_own(m, d).start()
+
     slots = 3 * (nz - 1)
     work = [functools.partial(give, xi) for xi in range(nx)] + [functools.partial(keep, xi) for xi in range(nx)]
     plan = list(enumerate(work, 1))
@@ -338,7 +364,18 @@
 
     def ring(s, carry):
         for idx, m in enumerate(order):
-            rs_chunk(m, s, False)
+            if m == 2:
+
+                @pl.when(s <= nz - 3)
+                def _():
+                    rs_chunk(2, s + 1, False)
+
+                @pl.when(s == nz - 2)
+                def _():
+                    finish(2)
+
+            else:
+                rs_chunk(m, s, False)
             for k in range(1, nz - 1):
                 fs = [f for slot, f in plan if slot == 3 * k + idx]
                 if fs:
@@ -355,32 +392,20 @@
         if slot >= slots:
             f()
 
-    spare = (nz - 1) % 2
-
-    def fin_copy(m, d, k):
-        to = lax.rem(me + k, nd)
-        return rcopy(zsend.at[m, d, spare, sized(to * dp, dp), :], outs[m].at[:, sized(me * fo + d * hf, hf)],
-                     fa_s.at[m, d, k - 1], fa_r.at[m, d, k - 1], {"data": to})
+    finish(0)
+    finish(1)
 
     for m in order:
-        for d in (0, 1):
-            val = part(m, d, z)
-            rs_copy(m, d, nz - 2).wait_recv()
-            rs_copy(m, d, nz - 3).wait_send()
-            zsend[m, d, spare] = (val + zrecv[m, d, nz % 2]).T
-            for k in range(1, nd):
-                fin_copy(m, d, k).start()
-            outs[m][:, sized(me * fo + d * hf, hf)] = zsend[m, d, spare, sized(me * dp, dp), :]
-
-    for m in order:
-        for k in range(1, nd):
-            frm = lax.rem(me + nd - k, nd)
+        for g, e in far:
+            frm, back_g = place(g, e), (nx - g) % nx
             for d in (0, 1):
                 dst = outs[m].at[:, sized(frm * fo + d * hf, hf)]
-                rcopy(dst, dst, fa_s.at[m, d, k - 1], fa_r.at[m, d, k - 1], {"data": frm}).wait_recv()
-                fin_copy(m, d, k).wait_send()
+                rcopy(dst, dst, fa_s.at[m, d, back_g, e], fa_r.at[m, d, back_g, e], {"data": frm}).wait_recv()
+                fin_copy(m, d, g, e).wait_send()
+        for k in range(1, nd):
             a2a(m, k).wait_send()
         for d in (0, 1):
+            fin_own(m, d).wait()
             rs_copy(m, d, nz - 2).wait_send()
     for q in range(4):
         for d in (0, 1):
@@ -404,6 +429,11 @@
         ex_copy(arr, nx - 1).wait_send()
 
 
+def hand_on(*refs):
+    for src, dst in zip(refs[:5], refs[5:]):
+        dst[...] = src[...]
+
+
 def solution(mesh):
     nz, ny, nd = mesh.shape["datb"], mesh.shape["model"], mesh.shape["data"]
     nx = nd // CORES
@@ -422,7 +452,7 @@
             functools.partial(kernel, nz, ny, nx),
             out_shape=[jax.ShapeDtypeStruct((r, d_model), BF)] * 2 + [jax.ShapeDtypeStruct((dp, fp), F32)] * 3,
             in_specs=[hbm] * 5,
-            out_specs=[vmem] * 5,
+            out_specs=[vmem] * 2 + [hbm] * 3,
             scratch_shapes=[
                 pltpu.VMEM((nx, CORES, br, d_model), BF),
                 pltpu.VMEM((nx, CORES, br, d_model), BF),
@@ -448,11 +478,18 @@
                 dma((2, nx)), dma((2, nx)),
                 dma((2, 2, most)), dma((2, 2, most)),
                 dma((2, 2, most)), dma((2, 2, most)),
-                dma((3, 2, nd - 1)), dma((3, 2, nd - 1)),
+                dma((3, 2, nx, CORES)), dma((3, 2, nx, CORES)), dma((3, 2)),
             ],
             compiler_params=pltpu.CompilerParams(collective_id=0, has_side_effects=True, vmem_limit_bytes=67043328),
             name="swiglu_step",
         )(tok_loc, grad_loc, wg_loc, wu_loc, wd_loc.T)
+        out, gin, dg, du, dd = pl.pallas_call(
+            hand_on,
+            out_shape=[jax.ShapeDtypeStruct((r, d_model), BF)] * 2 + [jax.ShapeDtypeStruct((dp, fp), F32)] * 3,
+            in_specs=[vmem] * 5,
+            out_specs=[vmem] * 5,
+            name="hand_on",
+        )(out, gin, dg, du, dd)
         return out, gin, dg, du, dd.T
 
     return jax.shard_map(local_step, mesh=mesh, in_specs=(ROW_SPEC, GATE_SPEC, GATE_SPEC, DOWN_SPEC, ROW_SPEC), out_specs=(ROW_SPEC, ROW_SPEC, GATE_SPEC, GATE_SPEC, DOWN_SPEC), check_vma=False)

time: 231 us -> 225 us (0.974)
  local copies, waits for them, and re-layouts: 5.7 us -> 0 us
    unnamed x13 -> x0, local copies, waits for them, and re-layouts: 5.7 us -> none
    pallas_call x1, Pallas kernels: 225 us -> 221 us  [local_step(): pl.pallas_call(functools.partial(kernel, nz, ny, nx), out_shape=[jax.Shap...]
    pallas_call x0 -> x1, Pallas kernels: none -> 2.85 us  [local_step(): pl.pallas_call(hand_on, out_shape=[jax.ShapeDtypeStruct((r, d_model), BF)...]
where the time goes in v4:
time: 225 us
  Pallas kernels  224 us (100%)
    pallas_call x1, Pallas kernels, local_step(): pl.pallas_call(functools.partial(kernel, nz, ny, nx), out_shape=[jax.Shap...  221 us

profile of v4, /device:TPU:1, one launch (start us, length us, event | category | flops | bytes accessed | tf_op | source)
XLA Modules:
  0.0 224.9 jit_solution(424461795029439196)
XLA Ops:
  0.6 221.4 %swiglu_step.1 = (bf16[64,2048]{1,0:T(8,128)(2,1)}, bf16[64,2048]{1,0:T(8,128)(2,1)}, f32[32,4096]{1,0:T(8,128)}, f32[32,4096]{1,0:T(8,128)}, f32[32,4096]{1,0:T(8,128)}) custom-call(bf16[64,2048]{1,0:T(8,128)(2,1)} %tok_in.1, bf16[64,2048]{1,0:T(8,128)(2,1)} %grad_in.1, bf16[32,4096]{1,0:T(8,128)(2,1)} %wg_in.1, bf16[32,4096]{1,0:T(8,128)(2,1)} %wu_in.1, ...), custom_call_target="tpu_custom_call" | custom-call | tf_op jit(solution)/shard_map/swiglu_step/pallas_call | solution.py:451
  222.0 2.9 %hand_on.1 = (bf16[64,2048]{1,0:T(8,128)(2,1)}, bf16[64,2048]{1,0:T(8,128)(2,1)}, f32[32,4096]{1,0:T(8,128)}, f32[32,4096]{1,0:T(8,128)}, f32[32,4096]{1,0:T(8,128)}) custom-call(bf16[64,2048]{1,0:T(8,128)(2,1)} %get-tuple-element.15.refs_0_, bf16[64,2048]{1,0:T(8,128)(2,1)} %get-tuple-element.16.refs_1_, f32[32,4096]{1,0:T(8,128)} %get-tuple-element.17.refs_2_, ...), custom_call_target="tpu_custom_call" | custom-call | tf_op jit(solution)/shard_map/hand_on/pallas_call | solution.py:486

commit v5 on v4

--- a/solution.py
+++ b/solution.py
@@ -232,9 +232,7 @@
 
     order = (2, 0, 1)
     rs_chunk(2, 0, True)
-    lax.fori_loop(0, nd, backward_block, 0)
-    rs_chunk(2, 1, False)
-    lax.fori_loop(nd, nd * 2, backward_block, 0)
+    lax.fori_loop(0, nd * 2, backward_block, 0)
 
     cols = d_model // 4
 
@@ -350,14 +348,16 @@
     plan = list(enumerate(work, 1))
     at = 1 + len(work)
     for s in range(max(sa_n) + 1):
-        plan.append((at + 3 * s, functools.partial(sa_event, s)))
-    at += 3 * max(sa_n)
+        plan.append((at + 8 * s // 3, functools.partial(sa_event, s)))
+    at += 8 * max(sa_n) // 3
     for s in range(max(sb_n) + 1):
         plan.append((at + s, functools.partial(sb_event, s)))
     plan.append((at + max(sb_n), sb_finish))
 
     for idx in (1, 2):
         rs_chunk(order[idx], 0, True)
+        if idx == 1:
+            rs_chunk(2, 1, False)
         for slot, f in plan:
             if slot == idx:
                 f()

time: 225 us -> 224 us (level)
  no operation moved by 1% of the time
where the time goes in v5:
time: 224 us; the launch traced here: 223 us
  Pallas kernels  222 us (99%)
    pallas_call x1, Pallas kernels, local_step(): pl.pallas_call(functools.partial(kernel, nz, ny, nx), out_shape=[jax.Shap...  219 us

profile of v5, /device:TPU:1, one launch (start us, length us, event | category | flops | bytes accessed | tf_op | source)
XLA Modules:
  0.0 222.8 jit_solution(9277229420193852659)
XLA Ops:
  0.6 219.3 %swiglu_step.1 = (bf16[64,2048]{1,0:T(8,128)(2,1)}, bf16[64,2048]{1,0:T(8,128)(2,1)}, f32[32,4096]{1,0:T(8,128)}, f32[32,4096]{1,0:T(8,128)}, f32[32,4096]{1,0:T(8,128)}) custom-call(bf16[64,2048]{1,0:T(8,128)(2,1)} %tok_in.1, bf16[64,2048]{1,0:T(8,128)(2,1)} %grad_in.1, bf16[32,4096]{1,0:T(8,128)(2,1)} %wg_in.1, bf16[32,4096]{1,0:T(8,128)(2,1)} %wu_in.1, ...), custom_call_target="tpu_custom_call" | custom-call | tf_op jit(solution)/shard_map/swiglu_step/pallas_call | solution.py:451
  220.0 2.9 %hand_on.1 = (bf16[64,2048]{1,0:T(8,128)(2,1)}, bf16[64,2048]{1,0:T(8,128)(2,1)}, f32[32,4096]{1,0:T(8,128)}, f32[32,4096]{1,0:T(8,128)}, f32[32,4096]{1,0:T(8,128)}) custom-call(bf16[64,2048]{1,0:T(8,128)(2,1)} %get-tuple-element.15.refs_0_, bf16[64,2048]{1,0:T(8,128)(2,1)} %get-tuple-element.16.refs_1_, f32[32,4096]{1,0:T(8,128)} %get-tuple-element.17.refs_2_, ...), custom_call_target="tpu_custom_call" | custom-call | tf_op jit(solution)/shard_map/hand_on/pallas_call | solution.py:486
